TPU v7x, 32 devices: a whole 2x2x4 slice. The times are simulated.
32 devices in a mesh: gx: 4 (over z), gy: 4 (over y, x), gz: 2 (over core).
Axes of the slice: x: 2, y: 2, z: 4, core: 2. Of those that a mesh axis runs over, the one named last changes fastest.
Arguments:
- velocity: float32 [3, 32, 64, 256], P(None, 'gx', 'gy', 'gz'), may hold values from -6 to 6
- density: float32 [32, 64, 256], P('gx', 'gy', 'gz'), may hold values from 0 to 2
- offsets: int32 [3, 32, 64, 256], P(None, 'gx', 'gy', 'gz'), may hold values from -4 to 3
- eighths: int32 [3, 32, 64, 256], P(None, 'gx', 'gy', 'gz'), may hold values from 0 to 7
Outputs:
- new_velocity: float32 [3, 32, 64, 256], P(None, 'gx', 'gy', 'gz')
- new_density: float32 [32, 64, 256], P('gx', 'gy', 'gz')
- pressure: float32 [32, 64, 256], P('gx', 'gy', 'gz')
All inputs are finite; a program needn't handle non-finite values.
Results may differ from a plain program's by a relative error of at most 0.00002.
Values sent between devices are 32-bit elements; how exact they have to be, the bound alone decides.
A program may use at most 64 MiB of HBM per device.

v0:
```python
import functools

import jax
import jax.numpy as jnp
from jax import lax
from jax.experimental import pallas as pl
from jax.experimental.pallas import tpu as pltpu
from jax.sharding import PartitionSpec as P

MESH = pl.DeviceIdType.MESH
RELAX = (6.0 / 7.0) / 6.0
HALO = 4
XY = [(dx, dy) for dx in (-1, 0, 1) for dy in (-1, 0, 1) if (dx, dy) != (0, 0)]
FAR = [(dx, dy) for dx in (-2, -1, 0, 1, 2) for dy in (-1, 0, 1) if (dx, dy) != (0, 0)]


def lanes(shape):
    return lax.broadcasted_iota(jnp.int32, shape, len(shape) - 1)


def roll(x, shift, axis):
    shift = shift % x.shape[axis]
    return x if shift == 0 else pltpu.roll(x, shift, axis)


def inside(sizes, me, delta):
    ok = None
    for n, i, d in zip(sizes, me, delta):
        if d:
            one = (i + d >= 0) & (i + d < n)
            ok = one if ok is None else ok & one
    return ok


class Comm:
    def __init__(self, sizes, me, send, recv):
        self.sizes, self.me, self.send, self.recv = sizes, me, send, recv
        self.copies = []

    def add(self, delta, src, dst, slot):
        device = tuple(i + d for i, d in zip(self.me, delta))
        copy = pltpu.make_async_remote_copy(
            src_ref=src, dst_ref=dst, send_sem=self.send.at[slot], recv_sem=self.recv.at[slot],
            device_id=device, device_id_type=MESH,
        )
        to = inside(self.sizes, self.me, delta)
        source = inside(self.sizes, self.me, tuple(-d for d in delta))
        pl.when(to)(copy.start)
        self.copies.append((copy, to, source))

    def wait(self):
        for copy, to, source in self.copies:
            pl.when(source)(copy.wait_recv)
        for copy, to, source in self.copies:
            pl.when(to)(copy.wait_send)


def zero_if_missing(sizes, me, delta, ref):
    @pl.when(jnp.logical_not(inside(sizes, me, delta)))
    def _():
        ref[...] = jnp.zeros(ref.shape, ref.dtype)


def pick_x(d):
    return {-1: 0, 1: 1}[d]


def exchange_xy(sizes, me, own, strips, rx, ry, rc, sems, out, meanwhile=None):
    f, p, r, _ = own.shape
    for i in range(p):
        strips[0, :, i] = own[:, i, 0:HALO, :]
        strips[1, :, i] = own[:, i, r - HALO : r, :]
    comm = Comm(sizes, me, *sems)
    for slot, (dx, dy) in enumerate(XY):
        xs = slice(0, HALO) if dx < 0 else slice(p - HALO, p)
        if dy == 0:
            src, dst = own.at[:, xs], rx.at[pick_x(-dx)]
        elif dx == 0:
            src, dst = strips.at[pick_x(dy)], ry.at[pick_x(-dy)]
        else:
            src, dst = strips.at[pick_x(dy), :, xs], rc.at[pick_x(-dx), pick_x(-dy)]
        comm.add((dx, dy, 0), src, dst, slot)
    for dx, dy in XY:
        ref = rx.at[pick_x(dx)] if dy == 0 else ry.at[pick_x(dy)] if dx == 0 else rc.at[pick_x(dx), pick_x(dy)]
        zero_if_missing(sizes, me, (dx, dy, 0), ref)
    out[:, HALO : HALO + p, HALO : HALO + r, :] = own[...]
    if meanwhile is not None:
        meanwhile()
    comm.wait()
    for sx, xs in ((0, slice(0, HALO)), (1, slice(HALO + p, HALO + p + HALO))):
        out[:, xs, HALO : HALO + r, :] = rx[sx]
        for sy, ys in ((0, slice(0, HALO)), (1, slice(HALO + r, HALO + r + HALO))):
            out[:, xs, ys, :] = rc[sx, sy]
    for sy, ys in ((0, slice(0, HALO)), (1, slice(HALO + r, HALO + r + HALO))):
        out[:, HALO : HALO + p, ys, :] = ry[sy]


def exchange_z(sizes, me, own, got, sems):
    comm = Comm(sizes, me, *sems)
    comm.add((0, 0, -1), own, got.at[1], 0)
    comm.add((0, 0, 1), own, got.at[0], 1)
    zero_if_missing(sizes, me, (0, 0, -1), got.at[0])
    zero_if_missing(sizes, me, (0, 0, 1), got.at[1])
    comm.wait()


def pack_z(ext, packed):
    f, p, rows, _ = ext.shape
    lane = lanes((rows, 128))
    for c in range(f):
        total = roll(ext[c, 0], 4, 1)
        for x in range(1, p):
            total = jnp.where(lane >= 8 * x, roll(ext[c, x], 4 + 8 * x, 1), total)
        packed[c] = total


def gather(x, index):
    return jnp.take_along_axis(x, index, axis=1, mode="promise_in_bounds")


def advect_tile(code, load, shift):
    ox, oy, oz = code & 7, (code >> 3) & 7, (code >> 6) & 7
    fx = ((code >> 9) & 7).astype(jnp.float32) * 0.125
    fy = ((code >> 12) & 7).astype(jnp.float32) * 0.125
    fz = ((code >> 15) & 7).astype(jnp.float32) * 0.125
    low = (lanes((8, 128)) + oz + shift) & 127
    high = (low + 1) & 127

    def weight(o, frac, step):
        return jnp.where(o == step, 1.0 - frac, jnp.where(o == step - 1, frac, 0.0))

    wy = [weight(oy, fy, dy) for dy in range(9)]
    totals = [None] * 4
    for dx in range(9):
        wx = weight(ox, fx, dx)
        wx0, wx1 = wx * (1.0 - fz), wx * fz
        for c in range(4):
            a0 = a1 = None
            for dy in range(9):
                rows = load(c, dx, dy)
                g0, g1 = wy[dy] * gather(rows, low), wy[dy] * gather(rows, high)
                a0 = g0 if a0 is None else a0 + g0
                a1 = g1 if a1 is None else a1 + g1
            value = wx0 * a0 + wx1 * a1
            totals[c] = value if totals[c] is None else totals[c] + value
    return totals


def kernel(sizes, vel, den, off_hbm, eig_hbm, new_vel, new_den, press, off, eig, fetch_sem, fields, stripA, rxA, ryA, rcA, ext, packed,
           gotP, srcA, srcB, code, codeB, resB, u, stripB, rxB, ryB, rcB, extU, packU, gotU, wide, s0, q0, r0,
           tmp0, own1, strip1, rx1, ry1, rc1, ext1, got1, wide1, q1, r1, tmp1, own2, got2, ext2, gotz2, sum1, fine,
           sxyA, rxyA, szA, rzA, sxyB, rxyB, szB, rzB, sxy1, rxy1, sz1, rz1, sxy2, rxy2, sz2, rz2):
    me = tuple(lax.axis_index(a) for a in ("gx", "gy", "gz"))
    p, r = den.shape[0], den.shape[1]
    fetch = [pltpu.make_async_copy(off_hbm, off, fetch_sem.at[0]), pltpu.make_async_copy(eig_hbm, eig, fetch_sem.at[1])]
    for copy in fetch:
        copy.start()
    fields[0:3] = vel[...]
    fields[3] = den[...]

    barrier = pltpu.get_barrier_semaphore()
    peers = [(dx, dy, 0) for dx, dy in FAR] + [(0, 0, -1), (0, 0, 1)]
    count = jnp.int32(0)
    for delta in peers:
        ok = inside(sizes, me, delta)

        @pl.when(ok)
        def _():
            pl.semaphore_signal(barrier, inc=1, device_id=tuple(i + d for i, d in zip(me, delta)), device_id_type=MESH)

        count = count + jnp.where(ok, 1, 0)
    pl.semaphore_wait(barrier, count)

    def positions():
        for copy in fetch:
            copy.wait()
        whole = (off[0] + 4) + 8 * (off[1] + 4) + 64 * (off[2] + 4)
        code[...] = whole + 512 * eig[0] + 4096 * eig[1] + 32768 * eig[2]
        lane16 = lanes((r, 128))
        total = roll(code[0], 12, 1)
        for g in range(1, p):
            total = jnp.where(lane16 >= 16 * g, roll(code[g], 16 * g + 12, 1), total)
        codeB[...] = total

    exchange_xy(sizes, me, fields, stripA, rxA, ryA, rcA, (sxyA, rxyA), ext, positions)
    pack_z(ext, packed)
    exchange_z(sizes, me, packed, gotP, (szA, rzA))

    rows = r + 8
    lane16 = lanes((r, 128))
    lane = lanes((rows, 128))
    for c in range(4):
        below, above = gotP[0, c], gotP[1, c]
        halves = []
        for h in range(2):
            total = None
            for g in range(8):
                x = 8 * h + g
                main = ext[c, x]
                srcA[c, x] = jnp.where(lane < 4, roll(below, -8 * x, 1), roll(main, 4, 1))
                piece = jnp.where((lane & 15) < 12, roll(main, 16 * g + 12, 1), roll(above, 8 * g + 8 - 64 * h, 1))
                total = piece if total is None else jnp.where(lane >= 16 * g, piece, total)
            halves.append(total)
        for dx in range(9):
            if dx == 8:
                srcB[c, dx] = halves[1]
            else:
                srcB[c, dx] = jnp.where(lane < 128 - 16 * dx, roll(halves[0], -16 * dx, 1), roll(halves[1], -16 * dx, 1))

    for half in range(r // 8):
        y0 = 8 * half
        totals = advect_tile(codeB[y0 : y0 + 8], lambda c, dx, dy: srcB[c, dx, y0 + dy : y0 + dy + 8, :], -4)
        for c in range(4):
            resB[c, y0 : y0 + 8] = totals[c]

    for half in range(r // 8):
        y0 = 8 * half

        def plane(x, carry, y0=y0):
            totals = advect_tile(code[x, y0 : y0 + 8], lambda c, dx, dy: srcA[c, x + dx, y0 + dy : y0 + dy + 8, :], 0)
            for c in range(4):
                u[c, x, y0 : y0 + 8] = totals[c]
            return carry

        lax.fori_loop(0, p, plane, 0)
    for c in range(4):
        for x in range(p):
            u[c, x] = jnp.where(lane16 >= 120, roll(resB[c], -(16 * x + 12), 1), u[c, x])
    new_den[...] = u[3]

    vel_u = u.at[0:3]
    exchange_xy(sizes, me, vel_u, stripB, rxB, ryB, rcB, (sxyB, rxyB), extU)
    pack_z(extU, packU)
    exchange_z(sizes, me, packU, gotU, (szB, rzB))
    for c in range(3):
        both = jnp.where((lane & 7) < 4, gotU[0, c], gotU[1, c])
        for x in range(p + 8):
            wide[c, x, :, 0:128] = extU[c, x]
            wide[c, x, :, 128:256] = roll(both, -(8 * x + 4), 1)

    def yz_mask(nrows, first_row, block_rows, cells):
        row = lax.broadcasted_iota(jnp.int32, (nrows, 256), 0) - first_row + me[1] * block_rows
        spot = lanes((nrows, 256))
        z = jnp.where(spot < 192, spot, spot - 256) + me[2] * cells
        return (row >= 0) & (row < sizes[1] * block_rows) & (z >= 0) & (z < sizes[2] * cells)

    def x_ok(x, first, block):
        g = x - first + me[0] * block
        return (g >= 0) & (g < sizes[0] * block)

    mask0 = yz_mask(rows, HALO, r, 128)

    def around(ref, x, step):
        v = ref[x]
        total = ref[x + 1] + ref[x - 1]
        total = total + roll(v, -1, 0) + roll(v, 1, 0)
        total = total + roll(v, -step, 1) + roll(v, step, 1)
        return 6.0 * v - total

    def second(ref, x, scale, step):
        v = ref[x]
        first = (RELAX * scale) * v
        return first + RELAX * (scale * v - (RELAX * scale) * around(ref, x, step))

    def source0(x, carry):
        part = wide[0, x + 1] - wide[0, x - 1]
        v = wide[1, x]
        part = part + (roll(v, -1, 0) - roll(v, 1, 0))
        v = wide[2, x]
        part = part + (roll(v, -1, 1) - roll(v, 1, 1))
        s0[x] = jnp.where(mask0 & x_ok(x, HALO, p), -0.5 * part, 0.0)
        return carry

    lax.fori_loop(1, p + 7, source0, 0)

    def second0(x, carry):
        q0[x] = jnp.where(mask0 & x_ok(x, HALO, p), second(s0, x, 1.0, 1), 0.0)
        return carry

    lax.fori_loop(2, p + 6, second0, 0)

    def residual0(x, carry):
        r0[x] = (s0[x] - around(q0, x, 1))[:, 0:128]
        return carry

    lax.fori_loop(HALO, HALO + p, residual0, 0)
    lane8 = lanes((r // 2, 128))
    for x in range(p // 2):
        tmp0[...] = r0[HALO + 2 * x] + r0[HALO + 2 * x + 1]
        v = tmp0[pl.ds(HALO, r // 2, stride=2), :] + tmp0[pl.ds(HALO + 1, r // 2, stride=2), :]
        v = v + jnp.where((lane8 & 1) == 0, roll(v, -1, 1), roll(v, 1, 1))
        own1[0, x] = 0.125 * v

    p1, r1n = p // 2, r // 2
    exchange_xy(sizes, me, own1, strip1, rx1, ry1, rc1, (sxy1, rxy1), ext1)
    exchange_z(sizes, me, ext1, got1, (sz1, rz1))
    rows1 = r1n + 8
    lane1 = lanes((rows1, 128))
    for x in range(p1 + 8):
        wide1[x, :, 0:128] = ext1[0, x]
        wide1[x, :, 128:256] = jnp.where(lane1 < 64, got1[1, 0, x], got1[0, 0, x])
    mask1 = yz_mask(rows1, HALO, r1n, 128)
    for x in range(HALO - 1, HALO + p1 + 1):
        q1[x] = jnp.where(mask1 & x_ok(x, HALO, p1), second(wide1, x, 4.0, 2), 0.0)
    for x in range(HALO, HALO + p1):
        r1[x] = (wide1[x] - 0.25 * around(q1, x, 2))[:, 0:128]
    p2, r2n = p1 // 2, r1n // 2
    lane4 = lanes((r2n, 128))
    for x in range(p2):
        tmp1[...] = r1[HALO + 2 * x] + r1[HALO + 2 * x + 1]
        v = tmp1[pl.ds(HALO, r2n, stride=2), :] + tmp1[pl.ds(HALO + 1, r2n, stride=2), :]
        v = v + jnp.where((lane4 & 3) < 2, roll(v, -2, 1), roll(v, 2, 1))
        own2[x] = 0.125 * v

    comm = Comm(sizes, me, sxy2, rxy2)
    for slot, (dx, dy) in enumerate(FAR):
        comm.add((dx, dy, 0), own2, got2.at[2 - dx, 1 - dy], slot)
    for dx, dy in FAR:
        zero_if_missing(sizes, me, (dx, dy, 0), got2.at[dx + 2, dy + 1])
    got2[2, 1] = own2[...]
    ext2[...] = jnp.zeros(ext2.shape, jnp.float32)
    comm.wait()
    for a in range(5):
        for b in range(3):
            ext2[p2 * a : p2 * a + p2, r2n * b : r2n * b + r2n, :] = got2[a, b]
    exchange_z(sizes, me, ext2, gotz2, (sz2, rz2))
    lane2 = lanes((16, 128))
    mask2 = yz_mask(16, r2n, r2n, 128)
    planes2 = {}
    for x in range(2 * p2 - 2, 3 * p2 + 2):
        planes2[x] = jnp.concatenate([ext2[x], jnp.where(lane2 < 64, gotz2[1, x], gotz2[0, x])], axis=1)
    sum1[...] = jnp.zeros(sum1.shape, jnp.float32)
    for x in range(2 * p2 - 1, 3 * p2 + 1):
        v = jnp.where(mask2 & x_ok(x, 2 * p2, p2), second(planes2, x, 16.0, 4), 0.0)
        first_row = r2n - 1
        take = r2n + 2
        base = HALO - 2
        for side in range(2):
            part = v[first_row : first_row + take, 128 * side : 128 * side + 128]
            sum1[x, side, pl.ds(base, take, stride=2), :] = part
            sum1[x, side, pl.ds(base + 1, take, stride=2), :] = part
    for x1 in range(HALO - 1, HALO + p1 + 1):
        x2 = (x1 - HALO) // 2 + 2 * p2
        for side in range(2):
            v = q1[x1, :, 128 * side : 128 * side + 128] + sum1[x2, side]
            part = v[HALO - 2 : HALO - 2 + r1n + 4]
            fine[x1, side, pl.ds(0, r1n + 4, stride=2), :] = part
            fine[x1, side, pl.ds(1, r1n + 4, stride=2), :] = part
    for x in range(HALO - 1, HALO + p + 1):
        x1 = (x - HALO) // 2 + HALO
        coarse = jnp.concatenate([fine[x1, 0], fine[x1, 1]], axis=1)
        s0[x] = jnp.where(mask0 & x_ok(x, HALO, p), q0[x] + coarse, 0.0)
    for x in range(p):
        v = s0[x + HALO]
        cut = lambda t: t[HALO : HALO + r, 0:128]
        press[x] = cut(v)
        new_vel[0, x] = u[0, x] - 0.5 * cut(s0[x + HALO + 1] - s0[x + HALO - 1])
        new_vel[1, x] = u[1, x] - 0.5 * cut(roll(v, -1, 0) - roll(v, 1, 0))
        new_vel[2, x] = u[2, x] - 0.5 * cut(roll(v, -1, 1) - roll(v, 1, 1))


def step(sizes, velocity, density, offsets, eighths):
    p, r, _ = density.shape
    f32 = jnp.float32

    def vm(*shape):
        return pltpu.VMEM(shape, f32)

    def xy(f, p, r):
        return [vm(2, f, p, 4, 128), vm(2, f, 4, r, 128), vm(2, f, p, 4, 128), vm(2, 2, f, 4, 4, 128)]

    p1, r1, p2, r2 = p // 2, r // 2, p // 4, r // 4
    rows, rows1 = r + 8, r1 + 8
    dma = lambda n: pltpu.SemaphoreType.DMA((n,))
    scratch = (
        [pltpu.VMEM(offsets.shape, jnp.int32), pltpu.VMEM(eighths.shape, jnp.int32), dma(2), vm(4, p, r, 128)] + xy(4, p, r)
        + [vm(4, p + 8, rows, 128), vm(4, rows, 128), vm(2, 4, rows, 128), vm(4, p + 8, rows, 128),
           vm(4, 9, rows, 128), pltpu.VMEM((p, r, 128), jnp.int32), pltpu.VMEM((r, 128), jnp.int32),
           vm(4, r, 128), vm(4, p, r, 128)]
        + xy(3, p, r)
        + [vm(3, p + 8, rows, 128), vm(3, rows, 128), vm(2, 3, rows, 128), vm(3, p + 8, rows, 256),
           vm(p + 8, rows, 256), vm(p + 8, rows, 256), vm(p + 8, rows, 128), vm(rows, 128), vm(1, p1, r1, 128)]
        + xy(1, p1, r1)
        + [vm(1, p1 + 8, rows1, 128), vm(2, 1, p1 + 8, rows1, 128), vm(p1 + 8, rows1, 256), vm(p1 + 8, rows1, 256),
           vm(p1 + 8, rows1, 128), vm(rows1, 128), vm(p2, r2, 128), vm(5, 3, p2, r2, 128), vm(5 * p2, 16, 128),
           vm(2, 5 * p2, 16, 128), vm(5 * p2, 2, rows1, 128), vm(p1 + 8, 2, rows, 128)]
        + [dma(8), dma(8), dma(2), dma(2)] * 3 + [dma(14), dma(14), dma(2), dma(2)]
    )
    vmem = pl.BlockSpec(memory_space=pltpu.VMEM)
    return pl.pallas_call(
        functools.partial(kernel, sizes),
        out_shape=(
            jax.ShapeDtypeStruct(velocity.shape, f32),
            jax.ShapeDtypeStruct(density.shape, f32),
            jax.ShapeDtypeStruct(density.shape, f32),
        ),
        in_specs=[vmem] * 2 + [pl.BlockSpec(memory_space=pltpu.HBM)] * 2,
        out_specs=(vmem,) * 3,
        scratch_shapes=scratch,
        compiler_params=pltpu.CompilerParams(
            collective_id=0, has_side_effects=True, vmem_limit_bytes=48 * 1024 * 1024
        ),
    )(velocity, density, offsets, eighths)


def solution(mesh):
    sizes = tuple(mesh.shape[a] for a in ("gx", "gy", "gz"))
    block = P("gx", "gy", "gz")
    stacked = P(None, "gx", "gy", "gz")
    return jax.shard_map(
        functools.partial(step, sizes),
        mesh=mesh,
        in_specs=(stacked, block, stacked, stacked),
        out_specs=(stacked, block, block),
        check_vma=False,
    )
```

profile of v0, /device:TPU:0, one launch (start us, length us, event | category | flops | bytes accessed | tf_op | source)
XLA Modules:
  0.0 58.2 jit_solution(7556223457951822451)
XLA Ops:
  0.6 0.0 copy-start
  0.6 0.9 %copy-done = f32[3,8,16,128]{3,2,1,0:T(8,128)S(1)} copy-done((f32[3,8,16,128]{3,2,1,0:T(8,128)S(1)}, f32[3,8,16,128]{3,2,1,0:T(8,128)}, u32[]{:S(2)}) %copy-start) | copy-done | bytes 196632
  1.6 0.0 copy-start.1
  1.6 0.9 %copy-done.1 = s32[3,8,16,128]{3,2,1,0:T(8,128)S(1)} copy-done((s32[3,8,16,128]{3,2,1,0:T(8,128)S(1)}, s32[3,8,16,128]{3,2,1,0:T(8,128)}, u32[]{:S(2)}) %copy-start.1) | copy-done | bytes 196632
  2.5 0.0 copy-start.2
  2.5 0.9 %copy-done.2 = s32[3,8,16,128]{3,2,1,0:T(8,128)S(1)} copy-done((s32[3,8,16,128]{3,2,1,0:T(8,128)S(1)}, s32[3,8,16,128]{3,2,1,0:T(8,128)}, u32[]{:S(2)}) %copy-start.2) | copy-done | bytes 196632
  3.4 0.0 copy-start.3
  3.4 0.8 %copy-done.3 = f32[8,16,128]{2,1,0:T(8,128)S(1)} copy-done((f32[8,16,128]{2,1,0:T(8,128)S(1)}, f32[8,16,128]{2,1,0:T(8,128)}, u32[]{:S(2)}) %copy-start.3) | copy-done | bytes 65560
  4.3 52.0 %shard_map.67 = (f32[3,8,16,128]{3,2,1,0:T(8,128)S(1)}, f32[8,16,128]{2,1,0:T(8,128)S(1)}, f32[8,16,128]{2,1,0:T(8,128)S(1)}) custom-call(f32[3,8,16,128]{3,2,1,0:T(8,128)S(1)} %copy-done, f32[8,16,128]{2,1,0:T(8,128)S(1)} %copy-done.3, s32[3,8,16,128]{3,2,1,0:T(8,128)S(1)} %copy-done.1, s32[3,8,16,128]{3,2,1,0:T(8,128)S(1)} %copy-done.2), custom_call_target="tpu_custom_call" | custom-call | tf_op jit(solution)/shard_map/pallas_call | solution.py:390
  56.3 0.7 %copy.10 = f32[3,8,16,128]{3,2,1,0:T(8,128)} copy(f32[3,8,16,128]{3,2,1,0:T(8,128)S(1)} %get-tuple-element.6) | data formatting | bytes 393216
  57.0 0.6 %copy.11 = f32[8,16,128]{2,1,0:T(8,128)} copy(f32[8,16,128]{2,1,0:T(8,128)S(1)} %get-tuple-element.7) | data formatting | bytes 131072
  57.6 0.6 %copy.12 = f32[8,16,128]{2,1,0:T(8,128)} copy(f32[8,16,128]{2,1,0:T(8,128)S(1)} %get-tuple-element.8) | data formatting | bytes 131072
Async XLA Ops:
  0.6 0.9 %copy-start = (f32[3,8,16,128]{3,2,1,0:T(8,128)S(1)}, f32[3,8,16,128]{3,2,1,0:T(8,128)}, u32[]{:S(2)}) copy-start(f32[3,8,16,128]{3,2,1,0:T(8,128)} %vel.1) | copy-start | bytes 589828
  1.6 0.9 %copy-start.1 = (s32[3,8,16,128]{3,2,1,0:T(8,128)S(1)}, s32[3,8,16,128]{3,2,1,0:T(8,128)}, u32[]{:S(2)}) copy-start(s32[3,8,16,128]{3,2,1,0:T(8,128)} %off_hbm.1) | copy-start | bytes 589828
  2.5 0.9 %copy-start.2 = (s32[3,8,16,128]{3,2,1,0:T(8,128)S(1)}, s32[3,8,16,128]{3,2,1,0:T(8,128)}, u32[]{:S(2)}) copy-start(s32[3,8,16,128]{3,2,1,0:T(8,128)} %eig_hbm.1) | copy-start | bytes 589828
  3.4 0.8 %copy-start.3 = (f32[8,16,128]{2,1,0:T(8,128)S(1)}, f32[8,16,128]{2,1,0:T(8,128)}, u32[]{:S(2)}) copy-start(f32[8,16,128]{2,1,0:T(8,128)} %den.1) | copy-start | bytes 196612
where the time goes:
time: 58.5 us; the launch traced here: 58.2 us
  Pallas kernels  52 us (89%)
  local copies, waits for them, and re-layouts  5.55 us (9%)
  between operations  0.65 us (1%)
    pallas_call x1, Pallas kernels, step(): pl.pallas_call(functools.partial(kernel, sizes), out_shape=(jax.ShapeDtyp...  52 us
    unnamed x11, local copies, waits for them, and re-layouts  5.55 us

commit v1 on v0

v1 whole, which is shorter than its diff:
```python
import functools

import jax
import jax.numpy as jnp
from jax import lax
from jax.experimental import pallas as pl
from jax.experimental.pallas import tpu as pltpu
from jax.sharding import PartitionSpec as P

MESH = pl.DeviceIdType.MESH
RELAX = (6.0 / 7.0) / 6.0
HALO = 4
XY = [(dx, dy) for dx in (-1, 0, 1) for dy in (-1, 0, 1) if (dx, dy) != (0, 0)]


def lanes(shape):
    return lax.broadcasted_iota(jnp.int32, shape, len(shape) - 1)


def roll(x, shift, axis):
    shift = shift % x.shape[axis]
    return x if shift == 0 else pltpu.roll(x, shift, axis)


def inside(sizes, me, delta):
    ok = None
    for n, i, d in zip(sizes, me, delta):
        if d:
            one = (i + d >= 0) & (i + d < n)
            ok = one if ok is None else ok & one
    return ok


class Comm:
    def __init__(self, sizes, me, send, recv):
        self.sizes, self.me, self.send, self.recv = sizes, me, send, recv
        self.copies = []

    def add(self, delta, src, dst, slot):
        device = tuple(i + d for i, d in zip(self.me, delta))
        copy = pltpu.make_async_remote_copy(
            src_ref=src, dst_ref=dst, send_sem=self.send.at[slot], recv_sem=self.recv.at[slot],
            device_id=device, device_id_type=MESH,
        )
        to = inside(self.sizes, self.me, delta)
        source = inside(self.sizes, self.me, tuple(-d for d in delta))
        pl.when(to)(copy.start)
        self.copies.append((copy, to, source))

    def wait(self):
        for copy, to, source in self.copies:
            pl.when(source)(copy.wait_recv)
        for copy, to, source in self.copies:
            pl.when(to)(copy.wait_send)


def zero_if_missing(sizes, me, delta, ref):
    @pl.when(jnp.logical_not(inside(sizes, me, delta)))
    def _():
        ref[...] = jnp.zeros(ref.shape, ref.dtype)


def pick_x(d):
    return {-1: 0, 1: 1}[d]


def exchange_xy(sizes, me, own, strips, rx, ry, rc, sems, out, meanwhile=None):
    f, p, r, _ = own.shape
    hx, hy = rx.shape[2], ry.shape[3]
    for i in range(p):
        strips[0, :, i] = own[:, i, 0:hy, :]
        strips[1, :, i] = own[:, i, r - hy : r, :]
    comm = Comm(sizes, me, *sems)
    for slot, (dx, dy) in enumerate(XY):
        xs = slice(0, hx) if dx < 0 else slice(p - hx, p)
        if dy == 0:
            src, dst = own.at[:, xs], rx.at[pick_x(-dx)]
        elif dx == 0:
            src, dst = strips.at[pick_x(dy)], ry.at[pick_x(-dy)]
        else:
            src, dst = strips.at[pick_x(dy), :, xs], rc.at[pick_x(-dx), pick_x(-dy)]
        comm.add((dx, dy, 0), src, dst, slot)
    for dx, dy in XY:
        ref = rx.at[pick_x(dx)] if dy == 0 else ry.at[pick_x(dy)] if dx == 0 else rc.at[pick_x(dx), pick_x(dy)]
        zero_if_missing(sizes, me, (dx, dy, 0), ref)
    out[:, HALO : HALO + p, HALO : HALO + r, :] = own[...]
    if meanwhile is not None:
        meanwhile()
    comm.wait()
    for sx, xs in ((0, slice(HALO - hx, HALO)), (1, slice(HALO + p, HALO + p + hx))):
        out[:, xs, HALO : HALO + r, :] = rx[sx]
        for sy, ys in ((0, slice(HALO - hy, HALO)), (1, slice(HALO + r, HALO + r + hy))):
            out[:, xs, ys, :] = rc[sx, sy]
    for sy, ys in ((0, slice(HALO - hy, HALO)), (1, slice(HALO + r, HALO + r + hy))):
        out[:, HALO : HALO + p, ys, :] = ry[sy]


class ZExchange:
    def __init__(self, sizes, me, own, got, sems):
        self.comm = Comm(sizes, me, *sems)
        self.comm.add((0, 0, -1), own, got.at[1], 0)
        self.comm.add((0, 0, 1), own, got.at[0], 1)
        zero_if_missing(sizes, me, (0, 0, -1), got.at[0])
        zero_if_missing(sizes, me, (0, 0, 1), got.at[1])
        self.wait = self.comm.wait


def swap_blocks(regs, width, shift=0):
    n = len(regs)
    lane = lanes(regs[0].shape)
    into, outof = ((lane + shift) & 127) // width, lane // width
    bits = [1 << k for k in range(n.bit_length() - 1)]
    for bit in bits:
        mask = (into & bit) != 0
        regs = [jnp.where(mask, regs[(i + bit) % n], regs[i]) for i in range(n)]
    regs = [roll(regs[i], width * i + shift, 1) for i in range(n)]
    regs = [regs[-i % n] for i in range(n)]
    for bit in bits:
        mask = (outof & bit) != 0
        regs = [jnp.where(mask, regs[(i - bit) % n], regs[i]) for i in range(n)]
    return regs


def pack_z(ext, packed):
    f, p, rows, _ = ext.shape
    lane = lanes((rows, 128))
    for c in range(f):
        total = roll(ext[c, 0], 4, 1)
        for x in range(1, p):
            total = jnp.where(lane >= 8 * x, roll(ext[c, x], 4 + 8 * x, 1), total)
        packed[c] = total


def gather(x, index):
    return jnp.take_along_axis(x, index, axis=1, mode="promise_in_bounds")


def advect_pair(code, load):
    lane = lanes((8, 128))
    part = (lane >> 3) & 1
    first = part == 0
    sums = []
    for half in range(2):
        v = jnp.where(first, code, roll(code, 8, 1)) if half == 0 else jnp.where(first, roll(code, -8, 1), code)
        ox, oy, oz = v & 7, (v >> 3) & 7, (v >> 6) & 7
        fx = ((v >> 9) & 7).astype(jnp.float32) * 0.125
        fy = ((v >> 12) & 7).astype(jnp.float32) * 0.125
        fz = ((v >> 15) & 7).astype(jnp.float32) * 0.125
        spot = (lane & 7) + oz + part
        near = spot < 8
        index = [((lane >> 4) + ox + cx) * 8 + (spot & 7) for cx in range(2)]
        wz = jnp.where(first, 1.0 - fz, fz)
        totals = [[None] * 2 for _ in range(4)]
        for dy in range(9):
            if dy == 0:
                wy = jnp.where(oy == 0, 1.0 - fy, 0.0)
            elif dy == 8:
                wy = jnp.where(oy == 7, fy, 0.0)
            else:
                wy = jnp.where(oy == dy, 1.0 - fy, jnp.where(oy == dy - 1, fy, 0.0))
            for c in range(4):
                one, two = load(c, half, dy), load(c, half + 1, dy)
                for cx in range(2):
                    value = wy * jnp.where(near, gather(one, index[cx]), gather(two, index[cx]))
                    totals[c][cx] = value if dy == 0 else totals[c][cx] + value
        wx0, wx1 = (1.0 - fx) * wz, fx * wz
        sums.append([wx0 * totals[c][0] + wx1 * totals[c][1] for c in range(4)])
    out = []
    for c in range(4):
        keep = jnp.where(first, sums[0][c], sums[1][c])
        move = jnp.where(first, sums[1][c], sums[0][c])
        out.append(keep + jnp.where(first, roll(move, -8, 1), roll(move, 8, 1)))
    return out


def kernel(sizes, vel_hbm, den_hbm, off_hbm, eig_hbm, new_vel, new_den, press, off, eig, fetch_sem, fields, stripA, rxA, ryA, rcA, ext,
           edge, gotP, src, code, codeT, resT, u, stripB, rxB, ryB, rcB, extU, packU, gotU, wide, s0, q0, r0,
           tmp0, own1, strip1, rx1, ry1, rc1, ext1, got1, wide1, q1, r1, tmp1, own2, got2, ext2, gotz2, sum1, fine,
           sxyA, rxyA, szA, rzA, sxyB, rxyB, szB, rzB, sxy1, rxy1, sz1, rz1, sxy2, rxy2, sz2, rz2):
    me = tuple(lax.axis_index(a) for a in ("gx", "gy", "gz"))
    p, r = fields.shape[1], fields.shape[2]
    pairs = [(vel_hbm, fields.at[0:3]), (den_hbm, fields.at[3]), (off_hbm, off), (eig_hbm, eig)]
    fetch = [pltpu.make_async_copy(a, b, fetch_sem.at[i]) for i, (a, b) in enumerate(pairs)]
    for copy in fetch:
        copy.start()

    barrier = pltpu.get_barrier_semaphore()
    peers = [(dx, dy, 0) for dx, dy in XY] + [(0, 0, -1), (0, 0, 1)]
    count = jnp.int32(0)
    for delta in peers:
        ok = inside(sizes, me, delta)

        @pl.when(ok)
        def _():
            pl.semaphore_signal(barrier, inc=1, device_id=tuple(i + d for i, d in zip(me, delta)), device_id_type=MESH)

        count = count + jnp.where(ok, 1, 0)
    for copy in fetch[:2]:
        copy.wait()
    pl.semaphore_wait(barrier, count)

    def positions():
        for copy in fetch[2:]:
            copy.wait()
        whole = (off[0] + 4) + 8 * (off[1] + 4) + 64 * (off[2] + 4)
        code[...] = whole + 512 * eig[0] + 4096 * eig[1] + 32768 * eig[2]
        for t in range(r // 8):
            for q, v in enumerate(swap_blocks([code[x, 8 * t : 8 * t + 8] for x in range(p)], 16)):
                codeT[t, q] = v

    exchange_xy(sizes, me, fields, stripA, rxA, ryA, rcA, (sxyA, rxyA), ext, positions)

    rows = r + 8
    tiles = rows // 8
    blocks = 128 // 8
    lane16 = lanes((r, 128))
    lane = lanes((rows, 128))

    def turn(c, carry):
        for t in range(tiles):
            for b, v in enumerate(swap_blocks([ext[c, x, 8 * t : 8 * t + 8] for x in range(p + 8)], 8, 4)):
                if b == 0:
                    edge[c, 8 * t : 8 * t + 8] = v
                else:
                    src[c, b, 8 * t : 8 * t + 8] = v
        return carry

    lax.fori_loop(0, 4, turn, 0)
    zA = ZExchange(sizes, me, edge, gotP, (szA, rzA))

    def advect(t, q):
        totals = advect_pair(codeT[t, q], lambda c, b, dy: src[c, 2 * q + b, 8 * t + dy : 8 * t + dy + 8, :])
        for c in range(4):
            resT[c, t, q] = totals[c]

    def middle(q, carry):
        for t in range(r // 8):
            advect(t, q)
        return carry

    lax.fori_loop(1, blocks // 2 - 1, middle, 0)
    zA.wait()
    low = (lane & 7) < 4
    for c in range(4):
        src[c, 0] = jnp.where(low, gotP[0, c], edge[c])
        src[c, blocks] = jnp.where(low, edge[c], gotP[1, c])

    def ends(i, carry):
        for t in range(r // 8):
            advect(t, i * (blocks // 2 - 1))
        return carry

    lax.fori_loop(0, 2, ends, 0)

    def back(c, carry):
        for t in range(r // 8):
            for x, v in enumerate(swap_blocks([resT[c, t, q] for q in range(blocks // 2)], 16)):
                u[c, x, 8 * t : 8 * t + 8] = v
        return carry

    lax.fori_loop(0, 4, back, 0)
    new_den[...] = u[3]

    vel_u = u.at[0:3]
    exchange_xy(sizes, me, vel_u, stripB, rxB, ryB, rcB, (sxyB, rxyB), extU)
    pack_z(extU, packU)
    ZExchange(sizes, me, packU, gotU, (szB, rzB)).wait()
    for c in range(3):
        both = jnp.where((lane & 7) < 4, gotU[0, c], gotU[1, c])
        for x in range(HALO - 3, HALO + p + 3):
            wide[c, x, :, 0:128] = extU[c, x]
            wide[c, x, :, 128:256] = roll(both, -(8 * x + 4), 1)

    def yz_mask(nrows, first_row, block_rows, cells):
        row = lax.broadcasted_iota(jnp.int32, (nrows, 256), 0) - first_row + me[1] * block_rows
        spot = lanes((nrows, 256))
        z = jnp.where(spot < 192, spot, spot - 256) + me[2] * cells
        return (row >= 0) & (row < sizes[1] * block_rows) & (z >= 0) & (z < sizes[2] * cells)

    def x_ok(x, first, block):
        g = x - first + me[0] * block
        return (g >= 0) & (g < sizes[0] * block)

    mask0 = yz_mask(rows, HALO, r, 128)

    def around(ref, x, step):
        v = ref[x]
        total = ref[x + 1] + ref[x - 1]
        total = total + roll(v, -1, 0) + roll(v, 1, 0)
        total = total + roll(v, -step, 1) + roll(v, step, 1)
        return 6.0 * v - total

    def second(ref, x, scale, step):
        v = ref[x]
        first = (RELAX * scale) * v
        return first + RELAX * (scale * v - (RELAX * scale) * around(ref, x, step))

    def source0(x, carry):
        part = wide[0, x + 1] - wide[0, x - 1]
        v = wide[1, x]
        part = part + (roll(v, -1, 0) - roll(v, 1, 0))
        v = wide[2, x]
        part = part + (roll(v, -1, 1) - roll(v, 1, 1))
        s0[x] = jnp.where(mask0 & x_ok(x, HALO, p), -0.5 * part, 0.0)
        return carry

    lax.fori_loop(HALO - 2, HALO + p + 2, source0, 0)

    def second0(x, carry):
        q0[x] = jnp.where(mask0 & x_ok(x, HALO, p), second(s0, x, 1.0, 1), 0.0)
        return carry

    lax.fori_loop(HALO - 1, HALO + p + 1, second0, 0)

    def residual0(x, carry):
        r0[x] = (s0[x] - around(q0, x, 1))[:, 0:128]
        return carry

    lax.fori_loop(HALO, HALO + p, residual0, 0)
    lane8 = lanes((r // 2, 128))
    for x in range(p // 2):
        tmp0[...] = r0[HALO + 2 * x] + r0[HALO + 2 * x + 1]
        v = tmp0[pl.ds(HALO, r // 2, stride=2), :] + tmp0[pl.ds(HALO + 1, r // 2, stride=2), :]
        v = v + jnp.where((lane8 & 1) == 0, roll(v, -1, 1), roll(v, 1, 1))
        own1[0, x] = 0.125 * v

    p1, r1n = p // 2, r // 2
    exchange_xy(sizes, me, own1, strip1, rx1, ry1, rc1, (sxy1, rxy1), ext1)
    near1 = pl.ds(HALO - 2, p1 + 4)
    ZExchange(sizes, me, ext1.at[0, near1], got1, (sz1, rz1)).wait()
    rows1 = r1n + 8
    lane1 = lanes((rows1, 128))
    for x in range(HALO - 2, HALO + p1 + 2):
        wide1[x, :, 0:128] = ext1[0, x]
        wide1[x, :, 128:256] = jnp.where(lane1 < 64, got1[1, x - HALO + 2], got1[0, x - HALO + 2])
    mask1 = yz_mask(rows1, HALO, r1n, 128)
    for x in range(HALO - 1, HALO + p1 + 1):
        q1[x] = jnp.where(mask1 & x_ok(x, HALO, p1), second(wide1, x, 4.0, 2), 0.0)
    for x in range(HALO, HALO + p1):
        r1[x] = (wide1[x] - 0.25 * around(q1, x, 2))[:, 0:128]
    p2, r2n = p1 // 2, r1n // 2
    lane4 = lanes((r2n, 128))
    for x in range(p2):
        tmp1[...] = r1[HALO + 2 * x] + r1[HALO + 2 * x + 1]
        v = tmp1[pl.ds(HALO, r2n, stride=2), :] + tmp1[pl.ds(HALO + 1, r2n, stride=2), :]
        v = v + jnp.where((lane4 & 3) < 2, roll(v, -2, 1), roll(v, 2, 1))
        own2[x] = 0.125 * v

    comm = Comm(sizes, me, sxy2, rxy2)
    for slot, (dx, dy) in enumerate(XY):
        comm.add((dx, dy, 0), own2, got2.at[1 - dx, 1 - dy], slot)
    for dx, dy in XY:
        zero_if_missing(sizes, me, (dx, dy, 0), got2.at[dx + 1, dy + 1])
    got2[1, 1] = own2[...]
    ext2[...] = jnp.zeros(ext2.shape, jnp.float32)
    comm.wait()
    for a in range(3):
        for b in range(3):
            ext2[p2 * a : p2 * a + p2, r2n * b : r2n * b + r2n, :] = got2[a, b]
    ZExchange(sizes, me, ext2, gotz2, (sz2, rz2)).wait()
    lane2 = lanes((16, 128))
    mask2 = yz_mask(16, r2n, r2n, 128)
    planes2 = {}
    for x in range(p2 - 2, 2 * p2 + 2):
        planes2[x] = jnp.concatenate([ext2[x], jnp.where(lane2 < 64, gotz2[1, x], gotz2[0, x])], axis=1)
    sum1[...] = jnp.zeros(sum1.shape, jnp.float32)
    for x in range(p2 - 1, 2 * p2 + 1):
        v = jnp.where(mask2 & x_ok(x, p2, p2), second(planes2, x, 16.0, 4), 0.0)
        first_row = r2n - 1
        take = r2n + 2
        base = HALO - 2
        for side in range(2):
            part = v[first_row : first_row + take, 128 * side : 128 * side + 128]
            sum1[x, side, pl.ds(base, take, stride=2), :] = part
            sum1[x, side, pl.ds(base + 1, take, stride=2), :] = part
    for x1 in range(HALO - 1, HALO + p1 + 1):
        x2 = (x1 - HALO) // 2 + p2
        for side in range(2):
            v = q1[x1, :, 128 * side : 128 * side + 128] + sum1[x2, side]
            part = v[HALO - 2 : HALO - 2 + r1n + 4]
            fine[x1, side, pl.ds(0, r1n + 4, stride=2), :] = part
            fine[x1, side, pl.ds(1, r1n + 4, stride=2), :] = part
    for x in range(HALO - 1, HALO + p + 1):
        x1 = (x - HALO) // 2 + HALO
        coarse = jnp.concatenate([fine[x1, 0], fine[x1, 1]], axis=1)
        s0[x] = jnp.where(mask0 & x_ok(x, HALO, p), q0[x] + coarse, 0.0)
    for x in range(p):
        v = s0[x + HALO]
        cut = lambda t: t[HALO : HALO + r, 0:128]
        press[x] = cut(v)
        new_vel[0, x] = u[0, x] - 0.5 * cut(s0[x + HALO + 1] - s0[x + HALO - 1])
        new_vel[1, x] = u[1, x] - 0.5 * cut(roll(v, -1, 0) - roll(v, 1, 0))
        new_vel[2, x] = u[2, x] - 0.5 * cut(roll(v, -1, 1) - roll(v, 1, 1))


def step(sizes, velocity, density, offsets, eighths):
    p, r, _ = density.shape
    f32 = jnp.float32

    def vm(*shape):
        return pltpu.VMEM(shape, f32)

    def xy(f, p, r, hx, hy):
        return [vm(2, f, p, hy, 128), vm(2, f, hx, r, 128), vm(2, f, p, hy, 128), vm(2, 2, f, hx, hy, 128)]

    assert p == 8 and r % 8 == 0
    p1, r1, p2, r2 = p // 2, r // 2, p // 4, r // 4
    rows, rows1 = r + 8, r1 + 8
    dma = lambda n: pltpu.SemaphoreType.DMA((n,))
    scratch = (
        [pltpu.VMEM(offsets.shape, jnp.int32), pltpu.VMEM(eighths.shape, jnp.int32), dma(4), vm(4, p, r, 128)] + xy(4, p, r, 4, 4)
        + [vm(4, p + 8, rows, 128), vm(4, rows, 128), vm(2, 4, rows, 128), vm(4, 17, rows, 128),
           pltpu.VMEM((p, r, 128), jnp.int32), pltpu.VMEM((r // 8, 8, 8, 128), jnp.int32),
           vm(4, r // 8, 8, 8, 128), vm(4, p, r, 128)]
        + xy(3, p, r, 3, 4)
        + [vm(3, p + 8, rows, 128), vm(3, rows, 128), vm(2, 3, rows, 128), vm(3, p + 8, rows, 256),
           vm(p + 8, rows, 256), vm(p + 8, rows, 256), vm(p + 8, rows, 128), vm(rows, 128), vm(1, p1, r1, 128)]
        + xy(1, p1, r1, 2, 2)
        + [vm(1, p1 + 8, rows1, 128), vm(2, p1 + 4, rows1, 128), vm(p1 + 8, rows1, 256), vm(p1 + 8, rows1, 256),
           vm(p1 + 8, rows1, 128), vm(rows1, 128), vm(p2, r2, 128), vm(3, 3, p2, r2, 128), vm(3 * p2, 16, 128),
           vm(2, 3 * p2, 16, 128), vm(3 * p2, 2, rows1, 128), vm(p1 + 8, 2, rows, 128)]
        + [dma(8), dma(8), dma(2), dma(2)] * 4
    )
    vmem = pl.BlockSpec(memory_space=pltpu.VMEM)
    return pl.pallas_call(
        functools.partial(kernel, sizes),
        out_shape=(
            jax.ShapeDtypeStruct(velocity.shape, f32),
            jax.ShapeDtypeStruct(density.shape, f32),
            jax.ShapeDtypeStruct(density.shape, f32),
        ),
        in_specs=[pl.BlockSpec(memory_space=pltpu.HBM)] * 4,
        out_specs=(vmem,) * 3,
        scratch_shapes=scratch,
        compiler_params=pltpu.CompilerParams(
            collective_id=0, has_side_effects=True, vmem_limit_bytes=60 * 1024 * 1024
        ),
    )(velocity, density, offsets, eighths)


def solution(mesh):
    sizes = tuple(mesh.shape[a] for a in ("gx", "gy", "gz"))
    block = P("gx", "gy", "gz")
    stacked = P(None, "gx", "gy", "gz")
    return jax.shard_map(
        functools.partial(step, sizes),
        mesh=mesh,
        in_specs=(stacked, block, stacked, stacked),
        out_specs=(stacked, block, block),
        check_vma=False,
    )
```

time: 58.5 us -> 51.2 us (0.88)
  Pallas kernels: 52 us -> 47.2 us
  local copies, waits for them, and re-layouts: 5.55 us -> 3.14 us
    pallas_call x1, Pallas kernels: 52 us -> 47.2 us  [step(): pl.pallas_call(functools.partial(kernel, sizes), out_shape=(jax.ShapeDtyp...]
    unnamed x11 -> x7, local copies, waits for them, and re-layouts: 5.55 us -> 3.14 us
where the time goes in v1:
time: 51.2 us; the launch traced here: 51 us
  Pallas kernels  47.2 us (92%)
  local copies, waits for them, and re-layouts  3.14 us (6%)
  between operations  0.65 us (1%)
    pallas_call x1, Pallas kernels, step(): pl.pallas_call(functools.partial(kernel, sizes), out_shape=(jax.ShapeDtyp...  47.2 us
    unnamed x7, local copies, waits for them, and re-layouts  3.14 us

profile of v1, /device:TPU:0, one launch (start us, length us, event | category | flops | bytes accessed | tf_op | source)
XLA Modules:
  0.0 51.0 jit_solution(8745923442284340826)
XLA Ops:
  0.6 47.2 %shard_map.67 = (f32[3,8,16,128]{3,2,1,0:T(8,128)}, f32[8,16,128]{2,1,0:T(8,128)}, f32[8,16,128]{2,1,0:T(8,128)}) custom-call(f32[3,8,16,128]{3,2,1,0:T(8,128)} %vel_hbm.1, f32[8,16,128]{2,1,0:T(8,128)} %den_hbm.1, s32[3,8,16,128]{3,2,1,0:T(8,128)} %off_hbm.1, s32[3,8,16,128]{3,2,1,0:T(8,128)} %eig_hbm.1), custom_call_target="tpu_custom_call" | custom-call | tf_op jit(solution)/shard_map/pallas_call | solution.py:425
  47.8 0.0 copy-start.1
  47.8 1.6 %copy.10 = f32[3,8,16,128]{3,2,1,0:T(8,128)} copy(f32[3,8,16,128]{3,2,1,0:T(8,128)} %get-tuple-element.6) | data formatting | bytes 393216
  49.5 0.0 copy-done.1
  49.5 0.0 copy-start
  49.5 0.6 %copy.11 = f32[8,16,128]{2,1,0:T(8,128)} copy(f32[8,16,128]{2,1,0:T(8,128)S(1)} %copy-done.1) | data formatting | bytes 131072
  50.1 0.2 copy-done
  50.3 0.6 %copy.12 = f32[8,16,128]{2,1,0:T(8,128)} copy(f32[8,16,128]{2,1,0:T(8,128)S(1)} %copy-done) | data formatting | bytes 131072
Async XLA Ops:
  47.8 1.7 %copy-start.1 = (f32[8,16,128]{2,1,0:T(8,128)S(1)}, f32[8,16,128]{2,1,0:T(8,128)}, u32[]{:S(2)}) copy-start(f32[8,16,128]{2,1,0:T(8,128)} %get-tuple-element.7) | copy-start | bytes 196612
  49.5 0.9 %copy-start = (f32[8,16,128]{2,1,0:T(8,128)S(1)}, f32[8,16,128]{2,1,0:T(8,128)}, u32[]{:S(2)}) copy-start(f32[8,16,128]{2,1,0:T(8,128)} %get-tuple-element.8) | copy-start | bytes 196612

commit v2 on v1

--- a/solution.py
+++ b/solution.py
@@ -135,42 +135,29 @@
     return jnp.take_along_axis(x, index, axis=1, mode="promise_in_bounds")
 
 
-def advect_pair(code, load):
+def advect_block(v, load):
     lane = lanes((8, 128))
     part = (lane >> 3) & 1
-    first = part == 0
-    sums = []
-    for half in range(2):
-        v = jnp.where(first, code, roll(code, 8, 1)) if half == 0 else jnp.where(first, roll(code, -8, 1), code)
-        ox, oy, oz = v & 7, (v >> 3) & 7, (v >> 6) & 7
-        fx = ((v >> 9) & 7).astype(jnp.float32) * 0.125
-        fy = ((v >> 12) & 7).astype(jnp.float32) * 0.125
-        fz = ((v >> 15) & 7).astype(jnp.float32) * 0.125
-        spot = (lane & 7) + oz + part
-        near = spot < 8
-        index = [((lane >> 4) + ox + cx) * 8 + (spot & 7) for cx in range(2)]
-        wz = jnp.where(first, 1.0 - fz, fz)
-        totals = [[None] * 2 for _ in range(4)]
-        for dy in range(9):
-            if dy == 0:
-                wy = jnp.where(oy == 0, 1.0 - fy, 0.0)
-            elif dy == 8:
-                wy = jnp.where(oy == 7, fy, 0.0)
-            else:
-                wy = jnp.where(oy == dy, 1.0 - fy, jnp.where(oy == dy - 1, fy, 0.0))
-            for c in range(4):
-                one, two = load(c, half, dy), load(c, half + 1, dy)
-                for cx in range(2):
-                    value = wy * jnp.where(near, gather(one, index[cx]), gather(two, index[cx]))
-                    totals[c][cx] = value if dy == 0 else totals[c][cx] + value
-        wx0, wx1 = (1.0 - fx) * wz, fx * wz
-        sums.append([wx0 * totals[c][0] + wx1 * totals[c][1] for c in range(4)])
-    out = []
-    for c in range(4):
-        keep = jnp.where(first, sums[0][c], sums[1][c])
-        move = jnp.where(first, sums[1][c], sums[0][c])
-        out.append(keep + jnp.where(first, roll(move, -8, 1), roll(move, 8, 1)))
-    return out
+    ox, oy, oz = v & 7, (v >> 3) & 7, (v >> 6) & 7
+    fx = ((v >> 9) & 7).astype(jnp.float32) * 0.125
+    fy = ((v >> 12) & 7).astype(jnp.float32) * 0.125
+    fz = ((v >> 15) & 7).astype(jnp.float32) * 0.125
+    spot = (lane & 7) + oz + part
+    near = spot < 8
+    first = ((lane >> 4) + ox) * 8 + (spot & 7)
+    wz = jnp.where(part == 0, 1.0 - fz, fz)
+    wy = [jnp.where(oy == dy, 1.0 - fy, jnp.where(oy == dy - 1, fy, 0.0)) for dy in range(9)]
+    totals = []
+    for cx in range(2):
+        index = first + 8 * cx
+        wx = (fx if cx else 1.0 - fx) * wz
+        for c in range(4):
+            total = None
+            for dy in range(9):
+                value = wy[dy] * jnp.where(near, gather(load(c, 0, dy), index), gather(load(c, 1, dy), index))
+                total = value if total is None else total + value
+            totals.append(wx * total)
+    return [totals[c] + totals[4 + c] for c in range(4)]
 
 
 def kernel(sizes, vel_hbm, den_hbm, off_hbm, eig_hbm, new_vel, new_den, press, off, eig, fetch_sem, fields, stripA, rxA, ryA, rcA, ext,
@@ -199,6 +186,8 @@
         copy.wait()
     pl.semaphore_wait(barrier, count)
 
+    even = ((lanes((8, 128)) >> 3) & 1) == 0
+
     def positions():
         for copy in fetch[2:]:
             copy.wait()
@@ -206,7 +195,8 @@
         code[...] = whole + 512 * eig[0] + 4096 * eig[1] + 32768 * eig[2]
         for t in range(r // 8):
             for q, v in enumerate(swap_blocks([code[x, 8 * t : 8 * t + 8] for x in range(p)], 16)):
-                codeT[t, q] = v
+                codeT[t, 2 * q] = jnp.where(even, v, roll(v, 8, 1))
+                codeT[t, 2 * q + 1] = jnp.where(even, roll(v, -8, 1), v)
 
     exchange_xy(sizes, me, fields, stripA, rxA, ryA, rcA, (sxyA, rxyA), ext, positions)
 
@@ -228,33 +218,35 @@
     lax.fori_loop(0, 4, turn, 0)
     zA = ZExchange(sizes, me, edge, gotP, (szA, rzA))
 
-    def advect(t, q):
-        totals = advect_pair(codeT[t, q], lambda c, b, dy: src[c, 2 * q + b, 8 * t + dy : 8 * t + dy + 8, :])
+    def advect(t, b):
+        totals = advect_block(codeT[t, b], lambda c, far, dy: src[c, b + far, 8 * t + dy : 8 * t + dy + 8, :])
         for c in range(4):
-            resT[c, t, q] = totals[c]
-
-    def middle(q, carry):
-        for t in range(r // 8):
-            advect(t, q)
-        return carry
-
-    lax.fori_loop(1, blocks // 2 - 1, middle, 0)
+            resT[c, t, b] = totals[c]
+
+    def middle(i, carry):
+        for half in range(2):
+            for t in range(r // 8):
+                advect(t, 2 * i + 1 + half)
+        return carry
+
+    lax.fori_loop(0, blocks // 2 - 1, middle, 0)
     zA.wait()
     low = (lane & 7) < 4
     for c in range(4):
         src[c, 0] = jnp.where(low, gotP[0, c], edge[c])
         src[c, blocks] = jnp.where(low, edge[c], gotP[1, c])
-
-    def ends(i, carry):
+    for b in (0, blocks - 1):
         for t in range(r // 8):
-            advect(t, i * (blocks // 2 - 1))
-        return carry
-
-    lax.fori_loop(0, 2, ends, 0)
+            advect(t, b)
 
     def back(c, carry):
         for t in range(r // 8):
-            for x, v in enumerate(swap_blocks([resT[c, t, q] for q in range(blocks // 2)], 16)):
+            pairs = []
+            for q in range(blocks // 2):
+                one, two = resT[c, t, 2 * q], resT[c, t, 2 * q + 1]
+                move = jnp.where(even, two, one)
+                pairs.append(jnp.where(even, one, two) + jnp.where(even, roll(move, -8, 1), roll(move, 8, 1)))
+            for x, v in enumerate(swap_blocks(pairs, 16)):
                 u[c, x, 8 * t : 8 * t + 8] = v
         return carry
 
@@ -410,8 +402,8 @@
     scratch = (
         [pltpu.VMEM(offsets.shape, jnp.int32), pltpu.VMEM(eighths.shape, jnp.int32), dma(4), vm(4, p, r, 128)] + xy(4, p, r, 4, 4)
         + [vm(4, p + 8, rows, 128), vm(4, rows, 128), vm(2, 4, rows, 128), vm(4, 17, rows, 128),
-           pltpu.VMEM((p, r, 128), jnp.int32), pltpu.VMEM((r // 8, 8, 8, 128), jnp.int32),
-           vm(4, r // 8, 8, 8, 128), vm(4, p, r, 128)]
+           pltpu.VMEM((p, r, 128), jnp.int32), pltpu.VMEM((r // 8, 16, 8, 128), jnp.int32),
+           vm(4, r // 8, 16, 8, 128), vm(4, p, r, 128)]
         + xy(3, p, r, 3, 4)
         + [vm(3, p + 8, rows, 128), vm(3, rows, 128), vm(2, 3, rows, 128), vm(3, p + 8, rows, 256),
            vm(p + 8, rows, 256), vm(p + 8, rows, 256), vm(p + 8, rows, 128), vm(rows, 128), vm(1, p1, r1, 128)]

time: 51.2 us -> 42.2 us (0.82)
  Pallas kernels: 47.2 us -> 38.2 us
    pallas_call x1, Pallas kernels: 47.2 us -> 38.2 us  [step(): pl.pallas_call(functools.partial(kernel, sizes), out_shape=(jax.ShapeDtyp...]
where the time goes in v2:
time: 42.2 us; the launch traced here: 42 us
  Pallas kernels  38.2 us (91%)
  local copies, waits for them, and re-layouts  3.14 us (7%)
  between operations  0.65 us (2%)
    pallas_call x1, Pallas kernels, step(): pl.pallas_call(functools.partial(kernel, sizes), out_shape=(jax.ShapeDtyp...  38.2 us
    unnamed x7, local copies, waits for them, and re-layouts  3.14 us

profile of v2, /device:TPU:0, one launch (start us, length us, event | category | flops | bytes accessed | tf_op | source)
XLA Modules:
  0.0 42.0 jit_solution(8984026272278474491)
XLA Ops:
  0.6 38.2 %shard_map.67 = (f32[3,8,16,128]{3,2,1,0:T(8,128)}, f32[8,16,128]{2,1,0:T(8,128)}, f32[8,16,128]{2,1,0:T(8,128)}) custom-call(f32[3,8,16,128]{3,2,1,0:T(8,128)} %vel_hbm.1, f32[8,16,128]{2,1,0:T(8,128)} %den_hbm.1, s32[3,8,16,128]{3,2,1,0:T(8,128)} %off_hbm.1, s32[3,8,16,128]{3,2,1,0:T(8,128)} %eig_hbm.1), custom_call_target="tpu_custom_call" | custom-call | tf_op jit(solution)/shard_map/pallas_call | solution.py:417
  38.8 0.0 copy-start.1
  38.8 1.6 %copy.10 = f32[3,8,16,128]{3,2,1,0:T(8,128)} copy(f32[3,8,16,128]{3,2,1,0:T(8,128)} %get-tuple-element.6) | data formatting | bytes 393216
  40.5 0.0 copy-done.1
  40.5 0.0 copy-start
  40.5 0.6 %copy.11 = f32[8,16,128]{2,1,0:T(8,128)} copy(f32[8,16,128]{2,1,0:T(8,128)S(1)} %copy-done.1) | data formatting | bytes 131072
  41.1 0.2 copy-done
  41.3 0.6 %copy.12 = f32[8,16,128]{2,1,0:T(8,128)} copy(f32[8,16,128]{2,1,0:T(8,128)S(1)} %copy-done) | data formatting | bytes 131072
Async XLA Ops:
  38.8 1.7 %copy-start.1 = (f32[8,16,128]{2,1,0:T(8,128)S(1)}, f32[8,16,128]{2,1,0:T(8,128)}, u32[]{:S(2)}) copy-start(f32[8,16,128]{2,1,0:T(8,128)} %get-tuple-element.7) | copy-start | bytes 196612
  40.5 0.9 %copy-start = (f32[8,16,128]{2,1,0:T(8,128)S(1)}, f32[8,16,128]{2,1,0:T(8,128)}, u32[]{:S(2)}) copy-start(f32[8,16,128]{2,1,0:T(8,128)} %get-tuple-element.8) | copy-start | bytes 196612

commit v3 on v2

v3 whole, which is shorter than its diff:
```python
import functools

import jax
import jax.numpy as jnp
from jax import lax
from jax.experimental import pallas as pl
from jax.experimental.pallas import tpu as pltpu
from jax.sharding import PartitionSpec as P

MESH = pl.DeviceIdType.MESH
RELAX = (6.0 / 7.0) / 6.0
HALO = 4
XY = [(-1, -1), (-1, 1), (1, -1), (1, 1), (-1, 0), (1, 0), (0, -1), (0, 1)]


def lanes(shape):
    return lax.broadcasted_iota(jnp.int32, shape, len(shape) - 1)


def roll(x, shift, axis):
    shift = shift % x.shape[axis]
    return x if shift == 0 else pltpu.roll(x, shift, axis)


def inside(sizes, me, delta):
    ok = None
    for n, i, d in zip(sizes, me, delta):
        if d:
            one = (i + d >= 0) & (i + d < n)
            ok = one if ok is None else ok & one
    return ok


class Comm:
    def __init__(self, sizes, me, send, recv):
        self.sizes, self.me, self.send, self.recv_sem = sizes, me, send, recv
        self.copies = []

    def add(self, delta, src, dst):
        slot = len(self.copies)
        device = tuple(i + d for i, d in zip(self.me, delta))
        copy = pltpu.make_async_remote_copy(
            src_ref=src, dst_ref=dst, send_sem=self.send.at[slot], recv_sem=self.recv_sem.at[slot],
            device_id=device, device_id_type=MESH,
        )
        to = inside(self.sizes, self.me, delta)
        source = inside(self.sizes, self.me, tuple(-d for d in delta))
        self.copies.append((copy, to, source, dst))

    def missing(self):
        for copy, to, source, dst in self.copies:

            @pl.when(jnp.logical_not(source))
            def _(dst=dst):
                dst[...] = jnp.zeros(dst.shape, dst.dtype)

    def start(self):
        for copy, to, source, dst in self.copies:
            pl.when(to)(copy.start)

    def recv(self, first=0, last=None):
        for copy, to, source, dst in self.copies[first:last]:
            pl.when(source)(copy.wait_recv)

    def sent(self):
        for copy, to, source, dst in self.copies:
            pl.when(to)(copy.wait_send)


def pick(d):
    return {-1: 0, 1: 1}[d]


def cut_strips(own, strips):
    f, p, r, _ = own.shape
    hy = strips.shape[3]
    for i in range(p):
        strips[0, :, i] = own[:, i, 0:hy, :]
        strips[1, :, i] = own[:, i, r - hy : r, :]


def add_xy(comm, own, strips, bufs, dz=0):
    rx, ry, rc = bufs
    p, hx = own.shape[1], rx.shape[2]
    for dx, dy in XY:
        xs = slice(0, hx) if dx < 0 else slice(p - hx, p)
        if dy == 0:
            src, dst = own.at[:, xs], rx.at[pick(-dx)]
        elif dx == 0:
            src, dst = strips.at[pick(dy)], ry.at[pick(-dy)]
        else:
            src, dst = strips.at[pick(dy), :, xs], rc.at[pick(-dx), pick(-dy)]
        comm.add((dx, dy, dz), src, dst)


def frame_halo(bufs, p, r, out):
    rx, ry, rc = bufs
    hx, hy = rx.shape[2], ry.shape[3]
    for sx, xs in ((0, slice(HALO - hx, HALO)), (1, slice(HALO + p, HALO + p + hx))):
        out[:, xs, HALO : HALO + r, :] = rx[sx]
        for sy, ys in ((0, slice(HALO - hy, HALO)), (1, slice(HALO + r, HALO + r + hy))):
            out[:, xs, ys, :] = rc[sx, sy]
    for sy, ys in ((0, slice(HALO - hy, HALO)), (1, slice(HALO + r, HALO + r + hy))):
        out[:, HALO : HALO + p, ys, :] = ry[sy]


def swap_blocks(regs, width, shift=0):
    n = len(regs)
    lane = lanes(regs[0].shape)
    into, outof = ((lane + shift) & 127) // width, lane // width
    bits = [1 << k for k in range(n.bit_length() - 1)]
    for bit in bits:
        mask = (into & bit) != 0
        regs = [jnp.where(mask, regs[(i + bit) % n], regs[i]) for i in range(n)]
    regs = [roll(regs[i], width * i + shift, 1) for i in range(n)]
    regs = [regs[-i % n] for i in range(n)]
    for bit in bits:
        mask = (outof & bit) != 0
        regs = [jnp.where(mask, regs[(i - bit) % n], regs[i]) for i in range(n)]
    return regs


def gather(x, index):
    return jnp.take_along_axis(x, index, axis=1, mode="promise_in_bounds")


def plan_block(v, place, weight):
    lane = lanes((8, 128))
    part = (lane >> 3) & 1
    ox, oy, oz = v & 7, (v >> 3) & 7, (v >> 6) & 7
    fx = ((v >> 9) & 7).astype(jnp.float32) * 0.125
    fy = ((v >> 12) & 7).astype(jnp.float32) * 0.125
    fz = ((v >> 15) & 7).astype(jnp.float32) * 0.125
    spot = (lane & 7) + oz + part
    place[0] = ((lane >> 4) + ox) * 8 + (spot & 7)
    place[1] = spot
    wz = jnp.where(part == 0, 1.0 - fz, fz)
    for dy in range(9):
        weight[dy] = jnp.where(oy == dy, 1.0 - fy, jnp.where(oy == dy - 1, fy, 0.0))
    weight[9] = (1.0 - fx) * wz
    weight[10] = fx * wz


def advect_block(place, weight, steps, load):
    near = place[1] < 8
    result = None
    for cx in range(2):
        index = place[0] + 8 * cx
        total = None
        for dy in steps:
            value = weight[dy] * jnp.where(near, gather(load(0, dy), index), gather(load(1, dy), index))
            total = value if total is None else total + value
        total = weight[9 + cx] * total
        result = total if result is None else result + total
    return result


def kernel(sizes, vel_hbm, den_hbm, off_hbm, eig_hbm, new_vel, new_den, press, off, eig, fetch_sem, fields, stripA, rxA, ryA, rcA, mixed,
           edge, gotP, src, code, place, weight, resT, u, extU, packU, wide, s0, q0, r0,
           tmp0, own1, strip1, rx1, ry1, rc1, rz1, ext1, wide1, q1, r1, tmp1, own2, got2, ext2, sum1, fine,
           sA, rA, szA, rzA, sB, rB, sC, rC, sD, rD, *bufB):
    me = tuple(lax.axis_index(a) for a in ("gx", "gy", "gz"))
    p, r = fields.shape[1], fields.shape[2]
    p1, r1n = p // 2, r // 2
    p2, r2n = p1 // 2, r1n // 2
    pairs = [(vel_hbm, fields.at[0:3]), (den_hbm, fields.at[3]), (off_hbm, off), (eig_hbm, eig)]
    fetch = [pltpu.make_async_copy(a, b, fetch_sem.at[i]) for i, (a, b) in enumerate(pairs)]
    for copy in fetch:
        copy.start()

    barrier = pltpu.get_barrier_semaphore()
    peers = [(dx, dy, dz) for dz in (-1, 0, 1) for dx in (-1, 0, 1) for dy in (-1, 0, 1) if (dx, dy, dz) != (0, 0, 0)]
    count = jnp.int32(0)
    for delta in peers:
        ok = inside(sizes, me, delta)

        @pl.when(ok)
        def _():
            pl.semaphore_signal(barrier, inc=1, device_id=tuple(i + d for i, d in zip(me, delta)), device_id_type=MESH)

        count = count + jnp.where(ok, 1, 0)

    sendA = [Comm(sizes, me, sA.at[i], rA.at[i]) for i in range(3)]
    for c in range(4):
        for dx in (-1, 1):
            xs = slice(0, HALO) if dx < 0 else slice(p - HALO, p)
            sendA[0].add((dx, 0, 0), fields.at[c, xs], rxA.at[pick(-dx), c])
            sendA[1].add((0, dx, 0), stripA.at[pick(dx), c], ryA.at[pick(-dx), c])
            for dy in (-1, 1):
                sendA[2].add((dx, dy, 0), stripA.at[pick(dy), c, xs], rcA.at[pick(-dx), pick(-dy), c])
    zA = Comm(sizes, me, szA, rzA)
    for c in range(4):
        zA.add((0, 0, -1), edge.at[c], gotP.at[1, c])
        zA.add((0, 0, 1), edge.at[c], gotP.at[0, c])
    fieldB = [bufB[8 * c : 8 * c + 8] for c in range(3)]
    commB = [Comm(sizes, me, sB.at[c], rB.at[c]) for c in range(3)]
    for c, (strip, rx, ry, rc, edgeB, estrB, ezB, ezyB) in enumerate(fieldB):
        add_xy(commB[c], u.at[c : c + 1], strip, (rx, ry, rc))
        for dz in (-1, 1):
            for dx in (-1, 1, 0):
                for dy in (-1, 1):
                    commB[c].add((dx, dy, dz), estrB.at[pick(dy)], ezyB.at[pick(-dz), 1 - dx, pick(-dy)])
                commB[c].add((dx, 0, dz), edgeB, ezB.at[pick(-dz), 1 - dx])
    commC = Comm(sizes, me, sC, rC)
    commD = Comm(sizes, me, sD, rD)
    for dz in (-1, 1, 0):
        add_xy(commC, own1, strip1, (rx1.at[1 - dz], ry1.at[1 - dz], rc1.at[1 - dz]), dz)
        for dx, dy in XY:
            commD.add((dx, dy, dz), own2, got2.at[1 - dz, 1 - dx, 1 - dy])
        if dz:
            commC.add((0, 0, dz), own1, rz1.at[pick(-dz)])
            commD.add((0, 0, dz), own2, got2.at[1 - dz, 1, 1])
    comms = sendA + [zA] + commB + [commC, commD]
    for comm in comms:
        comm.missing()
    ext2[...] = jnp.zeros(ext2.shape, jnp.float32)
    sum1[...] = jnp.zeros(sum1.shape, jnp.float32)
    for copy in fetch[:2]:
        copy.wait()
    cut_strips(fields, stripA)
    pl.semaphore_wait(barrier, count)
    for comm in sendA:
        comm.start()

    even = ((lanes((8, 128)) >> 3) & 1) == 0

    def positions():
        for copy in fetch[2:]:
            copy.wait()
        whole = (off[0] + 4) + 8 * (off[1] + 4) + 64 * (off[2] + 4)
        code[...] = whole + 512 * eig[0] + 4096 * eig[1] + 32768 * eig[2]
        for t in range(r // 8):
            for q, v in enumerate(swap_blocks([code[x, 8 * t : 8 * t + 8] for x in range(p)], 16)):
                code[q, 8 * t : 8 * t + 8] = v
        for t in range(r // 8):

            def plan(q, carry):
                v = code[q, 8 * t : 8 * t + 8]
                plan_block(jnp.where(even, v, roll(v, 8, 1)), place.at[t, 2 * q], weight.at[t, 2 * q])
                plan_block(jnp.where(even, roll(v, -8, 1), v), place.at[t, 2 * q + 1], weight.at[t, 2 * q + 1])
                return carry

            lax.fori_loop(0, 8, plan, 0)

    positions()
    rows = r + 8
    blocks = 128 // 8
    half = r // 8
    lane16 = lanes((r, 128))
    lane = lanes((rows, 128))
    near_steps = [[dy for dy in range(9) if 0 <= 8 * t + dy - 4 <= r - 8] for t in range(half)]
    far_steps = [[dy for dy in range(9) if dy not in near_steps[t]] for t in range(half)]

    def advect(c, t, b, steps):
        return advect_block(place.at[t, b], weight.at[t, b], steps, lambda far, dy: src[c, b + far, 8 * t + 4 + dy : 8 * t + 12 + dy, :])

    def put(c, b, start, size, v):
        if b == 0:
            edge[c, start : start + size] = v
        else:
            src[c, b, start : start + size] = v

    def first(c, carry):
        for dx in (-1, 1):
            xs = slice(0, HALO) if dx < 0 else slice(p - HALO, p)
            copy = pltpu.make_async_remote_copy(
                src_ref=fields.at[c, xs], dst_ref=rxA.at[pick(-dx), c], send_sem=sA.at[0, 2 * c + pick(dx)],
                recv_sem=rA.at[0, 2 * c + pick(dx)], device_id=tuple(i + d for i, d in zip(me, (dx, 0, 0))), device_id_type=MESH,
            )
            pl.when(inside(sizes, me, (-dx, 0, 0)))(copy.wait_recv)
        for t in range(half):
            ys = slice(8 * t, 8 * t + 8)
            planes = [rxA[0, c, x, ys] for x in range(HALO)] + [fields[c, x, ys] for x in range(p)] + [rxA[1, c, x, ys] for x in range(HALO)]
            for b, v in enumerate(swap_blocks(planes, 8, 4)):
                put(c, b, 8 + 8 * t, 8, v)
        for b in range(1, blocks - 1):
            for t in range(half):
                resT[c, t, b] = advect(c, t, b, near_steps[t])
        return carry

    lax.fori_loop(0, 4, first, 0)
    sendA[1].recv()
    sendA[2].recv()

    def turn(c, carry):
        for side, at in ((1, 0), (0, 4)):
            for x in range(HALO):
                mixed[c, x, at : at + 4] = rcA[0, side, c, x]
                mixed[c, HALO + p + x, at : at + 4] = rcA[1, side, c, x]
            for x in range(p):
                mixed[c, HALO + x, at : at + 4] = ryA[side, c, x]
        for b, v in enumerate(swap_blocks([mixed[c, x] for x in range(p + 8)], 8, 4)):
            put(c, b, 4, 4, v[4:8])
            put(c, b, r + 8, 4, v[0:4])
        return carry

    lax.fori_loop(0, 4, turn, 0)
    zA.start()
    low = (lanes((r + 16, 128)) & 7) < 4
    for c in range(4):
        for b in range(1, blocks - 1):
            for t in range(half):
                resT[c, t, b] = resT[c, t, b] + advect(c, t, b, far_steps[t])
        zA.recv(2 * c, 2 * c + 2)
        src[c, 0] = jnp.where(low, gotP[0, c], edge[c])
        src[c, blocks] = jnp.where(low, edge[c], gotP[1, c])
        for b in (0, blocks - 1):
            for t in range(half):
                resT[c, t, b] = advect(c, t, b, range(9))
        for t in range(half):
            pairs = []
            for q in range(blocks // 2):
                one, two = resT[c, t, 2 * q], resT[c, t, 2 * q + 1]
                move = jnp.where(even, two, one)
                pairs.append(jnp.where(even, one, two) + jnp.where(even, roll(move, -8, 1), roll(move, 8, 1)))
            for x, v in enumerate(swap_blocks(pairs, 16)):
                u[c, x, 8 * t : 8 * t + 8] = v
        if c == 3:
            new_den[...] = u[3]
            break
        strip, rx, ry, rc, edgeB, estrB, ezB, ezyB = fieldB[c]
        cut_strips(u.at[c : c + 1], strip)
        total = roll(u[c, 0], 4, 1)
        for x in range(1, p):
            total = jnp.where(lane16 >= 8 * x, roll(u[c, x], 4 + 8 * x, 1), total)
        edgeB[...] = total
        estrB[0] = total[0 : estrB.shape[1]]
        estrB[1] = total[r - estrB.shape[1] : r]
        commB[c].start()

    extU[:, HALO : HALO + p, HALO : HALO + r, :] = u[0:3]
    for c in range(3):
        commB[c].recv()

    def edges(lo, hi):
        spot = lanes(lo[0].shape)
        v = [jnp.where((spot & 7) < 4, lo[i], hi[i]) for i in range(3)]
        return jnp.where(spot < 32, roll(v[0], -32, 1), jnp.where(spot < 96, roll(v[1], 32, 1), roll(v[2], 96, 1)))

    for c, (strip, rx, ry, rc, edgeB, estrB, ezB, ezyB) in enumerate(fieldB):
        frame_halo((rx, ry, rc), p, r, extU.at[c : c + 1])
        hy = estrB.shape[1]
        packU[c, HALO : HALO + r] = edges([ezB[0, i] for i in range(3)], [ezB[1, i] for i in range(3)])
        for sy, ys in ((0, slice(HALO - hy, HALO)), (1, slice(HALO + r, HALO + r + hy))):
            packU[c, ys] = edges([ezyB[0, i, sy] for i in range(3)], [ezyB[1, i, sy] for i in range(3)])
    for c in range(3):
        for x in range(HALO - 3, HALO + p + 3):
            wide[c, x, :, 0:128] = extU[c, x]
            wide[c, x, :, 128:256] = roll(packU[c], -(8 * x + 4), 1)

    def yz_mask(nrows, first_row, block_rows, cells):
        row = lax.broadcasted_iota(jnp.int32, (nrows, 256), 0) - first_row + me[1] * block_rows
        spot = lanes((nrows, 256))
        z = jnp.where(spot < 192, spot, spot - 256) + me[2] * cells
        return (row >= 0) & (row < sizes[1] * block_rows) & (z >= 0) & (z < sizes[2] * cells)

    def x_ok(x, first, block):
        g = x - first + me[0] * block
        return (g >= 0) & (g < sizes[0] * block)

    mask0 = yz_mask(rows, HALO, r, 128)

    def around(ref, x, step):
        v = ref[x]
        total = ref[x + 1] + ref[x - 1]
        total = total + roll(v, -1, 0) + roll(v, 1, 0)
        total = total + roll(v, -step, 1) + roll(v, step, 1)
        return 6.0 * v - total

    def second(ref, x, scale, step):
        v = ref[x]
        first = (RELAX * scale) * v
        return first + RELAX * (scale * v - (RELAX * scale) * around(ref, x, step))

    def source0(x, carry):
        part = wide[0, x + 1] - wide[0, x - 1]
        v = wide[1, x]
        part = part + (roll(v, -1, 0) - roll(v, 1, 0))
        v = wide[2, x]
        part = part + (roll(v, -1, 1) - roll(v, 1, 1))
        s0[x] = jnp.where(mask0 & x_ok(x, HALO, p), -0.5 * part, 0.0)
        return carry

    lax.fori_loop(HALO - 2, HALO + p + 2, source0, 0)

    def second0(x, carry):
        q0[x] = jnp.where(mask0 & x_ok(x, HALO, p), second(s0, x, 1.0, 1), 0.0)
        return carry

    lax.fori_loop(HALO - 1, HALO + p + 1, second0, 0)

    def residual0(x, carry):
        r0[x] = (s0[x] - around(q0, x, 1))[:, 0:128]
        return carry

    lax.fori_loop(HALO, HALO + p, residual0, 0)
    lane8 = lanes((r // 2, 128))
    for x in range(p // 2):
        tmp0[...] = r0[HALO + 2 * x] + r0[HALO + 2 * x + 1]
        v = tmp0[pl.ds(HALO, r // 2, stride=2), :] + tmp0[pl.ds(HALO + 1, r // 2, stride=2), :]
        v = v + jnp.where((lane8 & 1) == 0, roll(v, -1, 1), roll(v, 1, 1))
        own1[0, x] = 0.125 * v

    cut_strips(own1, strip1)
    commC.start()
    commC.recv()
    rows1 = r1n + 8
    for dz in range(3):
        ext1[dz, :, HALO : HALO + p1, HALO : HALO + r1n, :] = own1[...] if dz == 1 else rz1[dz // 2]
        frame_halo((rx1.at[dz], ry1.at[dz], rc1.at[dz]), p1, r1n, ext1.at[dz])
    lane1 = lanes((rows1, 128))
    for x in range(HALO - 2, HALO + p1 + 2):
        wide1[x, :, 0:128] = ext1[1, 0, x]
        wide1[x, :, 128:256] = jnp.where(lane1 < 64, ext1[2, 0, x], ext1[0, 0, x])
    mask1 = yz_mask(rows1, HALO, r1n, 128)
    for x in range(HALO - 1, HALO + p1 + 1):
        q1[x] = jnp.where(mask1 & x_ok(x, HALO, p1), second(wide1, x, 4.0, 2), 0.0)
    for x in range(HALO, HALO + p1):
        r1[x] = (wide1[x] - 0.25 * around(q1, x, 2))[:, 0:128]
    lane4 = lanes((r2n, 128))
    for x in range(p2):
        tmp1[...] = r1[HALO + 2 * x] + r1[HALO + 2 * x + 1]
        v = tmp1[pl.ds(HALO, r2n, stride=2), :] + tmp1[pl.ds(HALO + 1, r2n, stride=2), :]
        v = v + jnp.where((lane4 & 3) < 2, roll(v, -2, 1), roll(v, 2, 1))
        own2[x] = 0.125 * v

    commD.start()
    got2[1, 1, 1] = own2[...]
    commD.recv()
    for z in range(3):
        for a in range(3):
            for b in range(3):
                ext2[z, p2 * a : p2 * a + p2, r2n * b : r2n * b + r2n, :] = got2[z, a, b]
    lane2 = lanes((16, 128))
    mask2 = yz_mask(16, r2n, r2n, 128)
    planes2 = {}
    for x in range(p2 - 2, 2 * p2 + 2):
        planes2[x] = jnp.concatenate([ext2[1, x], jnp.where(lane2 < 64, ext2[2, x], ext2[0, x])], axis=1)
    for x in range(p2 - 1, 2 * p2 + 1):
        v = jnp.where(mask2 & x_ok(x, p2, p2), second(planes2, x, 16.0, 4), 0.0)
        first_row = r2n - 1
        take = r2n + 2
        base = HALO - 2
        for side in range(2):
            part = v[first_row : first_row + take, 128 * side : 128 * side + 128]
            sum1[x, side, pl.ds(base, take, stride=2), :] = part
            sum1[x, side, pl.ds(base + 1, take, stride=2), :] = part
    for x1 in range(HALO - 1, HALO + p1 + 1):
        x2 = (x1 - HALO) // 2 + p2
        for side in range(2):
            v = q1[x1, :, 128 * side : 128 * side + 128] + sum1[x2, side]
            part = v[HALO - 2 : HALO - 2 + r1n + 4]
            fine[x1, side, pl.ds(0, r1n + 4, stride=2), :] = part
            fine[x1, side, pl.ds(1, r1n + 4, stride=2), :] = part
    for x in range(HALO - 1, HALO + p + 1):
        x1 = (x - HALO) // 2 + HALO
        coarse = jnp.concatenate([fine[x1, 0], fine[x1, 1]], axis=1)
        s0[x] = jnp.where(mask0 & x_ok(x, HALO, p), q0[x] + coarse, 0.0)
    for x in range(p):
        v = s0[x + HALO]
        cut = lambda t: t[HALO : HALO + r, 0:128]
        press[x] = cut(v)
        new_vel[0, x] = u[0, x] - 0.5 * cut(s0[x + HALO + 1] - s0[x + HALO - 1])
        new_vel[1, x] = u[1, x] - 0.5 * cut(roll(v, -1, 0) - roll(v, 1, 0))
        new_vel[2, x] = u[2, x] - 0.5 * cut(roll(v, -1, 1) - roll(v, 1, 1))
    for comm in comms:
        comm.sent()


def write_kernel(*refs):
    n = len(refs) // 2
    copies = [pltpu.make_async_copy(refs[i], refs[n + i], refs[-1].at[i]) for i in range(n)]
    for copy in copies:
        copy.start()
    for copy in copies:
        copy.wait()


def write_out(results):
    return pl.pallas_call(
        write_kernel,
        out_shape=tuple(jax.ShapeDtypeStruct(a.shape, a.dtype) for a in results),
        in_specs=[pl.BlockSpec(memory_space=pltpu.VMEM)] * len(results),
        out_specs=(pl.BlockSpec(memory_space=pltpu.HBM),) * len(results),
        scratch_shapes=[pltpu.SemaphoreType.DMA((len(results),))],
        compiler_params=pltpu.CompilerParams(vmem_limit_bytes=1 << 20),
    )(*results)


def step(sizes, velocity, density, offsets, eighths):
    p, r, _ = density.shape
    f32 = jnp.float32

    def vm(*shape):
        return pltpu.VMEM(shape, f32)

    def xy(f, p, r, hx, hy):
        return [vm(2, f, p, hy, 128), vm(2, f, hx, r, 128), vm(2, f, p, hy, 128), vm(2, 2, f, hx, hy, 128)]

    assert p == 8 and r % 8 == 0
    p1, r1, p2, r2 = p // 2, r // 2, p // 4, r // 4
    rows, rows1 = r + 8, r1 + 8
    dma = lambda *n: pltpu.SemaphoreType.DMA(n)
    half = r // 8
    scratch = (
        [pltpu.VMEM(offsets.shape, jnp.int32), pltpu.VMEM(eighths.shape, jnp.int32), dma(4), vm(4, p, r, 128)] + xy(4, p, r, 4, 4)
        + [vm(4, p + 8, 8, 128), vm(4, r + 16, 128), vm(2, 4, r + 16, 128), vm(4, 17, r + 16, 128),
           pltpu.VMEM((p, r, 128), jnp.int32), pltpu.VMEM((half, 16, 2, 8, 128), jnp.int32), vm(half, 16, 11, 8, 128),
           vm(4, half, 16, 8, 128), vm(4, p, r, 128)]
        + [vm(3, p + 8, rows, 128), vm(3, rows, 128), vm(3, p + 8, rows, 256),
           vm(p + 8, rows, 256), vm(p + 8, rows, 256), vm(p + 8, rows, 128), vm(rows, 128), vm(1, p1, r1, 128)]
        + [vm(2, 1, p1, 2, 128), vm(3, 2, 1, 2, r1, 128), vm(3, 2, 1, p1, 2, 128), vm(3, 2, 2, 1, 2, 2, 128), vm(2, 1, p1, r1, 128)]
        + [vm(3, 1, p1 + 8, rows1, 128), vm(p1 + 8, rows1, 256), vm(p1 + 8, rows1, 256),
           vm(p1 + 8, rows1, 128), vm(rows1, 128), vm(p2, r2, 128), vm(3, 3, 3, p2, r2, 128), vm(3, 3 * p2, 16, 128),
           vm(3 * p2, 2, rows1, 128), vm(p1 + 8, 2, rows, 128)]
        + [dma(3, 16), dma(3, 16), dma(8), dma(8), dma(3, 26), dma(3, 26)] + [dma(26), dma(26)] * 2
    )
    for hx, hy in ((3, 2), (2, 4), (2, 2)):
        scratch += xy(1, p, r, hx, hy) + [vm(r, 128), vm(2, hy, 128), vm(2, 3, r, 128), vm(2, 3, 2, hy, 128)]
    vmem = pl.BlockSpec(memory_space=pltpu.VMEM)
    results = pl.pallas_call(
        functools.partial(kernel, sizes),
        out_shape=(
            jax.ShapeDtypeStruct(velocity.shape, f32),
            jax.ShapeDtypeStruct(density.shape, f32),
            jax.ShapeDtypeStruct(density.shape, f32),
        ),
        in_specs=[pl.BlockSpec(memory_space=pltpu.HBM)] * 4,
        out_specs=(vmem,) * 3,
        scratch_shapes=scratch,
        compiler_params=pltpu.CompilerParams(
            collective_id=0, has_side_effects=True, vmem_limit_bytes=32 * 1024 * 1024
        ),
    )(*[pltpu.with_memory_space_constraint(a, pltpu.HBM) for a in (velocity, density, offsets, eighths)])
    return write_out(results)


def solution(mesh):
    sizes = tuple(mesh.shape[a] for a in ("gx", "gy", "gz"))
    block = P("gx", "gy", "gz")
    stacked = P(None, "gx", "gy", "gz")
    return jax.shard_map(
        functools.partial(step, sizes),
        mesh=mesh,
        in_specs=(stacked, block, stacked, stacked),
        out_specs=(stacked, block, block),
        check_vma=False,
    )
```

time: 42.2 us -> 36.8 us (0.87)
  local copies, waits for them, and re-layouts: 3.14 us -> 0 us
  Pallas kernels: 38.2 us -> 36.1 us
    unnamed x7 -> x0, local copies, waits for them, and re-layouts: 3.14 us -> none
    pallas_call x1, Pallas kernels: 38.2 us -> 35.3 us  [step(): pl.pallas_call(functools.partial(kernel, sizes), out_shape=(jax.ShapeDtyp...]
    pallas_call x0 -> x1, Pallas kernels: none -> 0.74 us  [write_out(): pl.pallas_call(write_kernel, out_shape=tuple((jax.ShapeDtypeStruct(a.shap...]
where the time goes in v3:
time: 36.8 us; the launch traced here: 36.7 us
  Pallas kernels  36.1 us (98%)
  between operations  0.64 us (2%)
    pallas_call x1, Pallas kernels, step(): pl.pallas_call(functools.partial(kernel, sizes), out_shape=(jax.ShapeDtyp...  35.3 us
    pallas_call x1, Pallas kernels, write_out(): pl.pallas_call(write_kernel, out_shape=tuple((jax.ShapeDtypeStruct(a.shap...  0.74 us

profile of v3, /device:TPU:0, one launch (start us, length us, event | category | flops | bytes accessed | tf_op | source)
XLA Modules:
  0.0 36.7 jit_solution(1096787633664943905)
XLA Ops:
  0.6 35.3 %shard_map.67 = (f32[3,8,16,128]{3,2,1,0:T(8,128)S(1)}, f32[8,16,128]{2,1,0:T(8,128)S(1)}, f32[8,16,128]{2,1,0:T(8,128)S(1)}) custom-call(f32[3,8,16,128]{3,2,1,0:T(8,128)} %vel_hbm.1, f32[8,16,128]{2,1,0:T(8,128)} %den_hbm.1, s32[3,8,16,128]{3,2,1,0:T(8,128)} %off_hbm.1, s32[3,8,16,128]{3,2,1,0:T(8,128)} %eig_hbm.1), custom_call_target="tpu_custom_call" | custom-call | tf_op jit(solution)/shard_map/pallas_call | solution.py:521
  36.0 0.7 %shard_map.68 = (f32[3,8,16,128]{3,2,1,0:T(8,128)}, f32[8,16,128]{2,1,0:T(8,128)}, f32[8,16,128]{2,1,0:T(8,128)}) custom-call(f32[3,8,16,128]{3,2,1,0:T(8,128)S(1)} %get-tuple-element.6.refs_0_, f32[8,16,128]{2,1,0:T(8,128)S(1)} %get-tuple-element.7.refs_1_, f32[8,16,128]{2,1,0:T(8,128)S(1)} %get-tuple-element.8.refs_2_), custom_call_target="tpu_custom_call" | custom-call | tf_op jit(solution)/shard_map/pallas_call | solution.py:480

commit v4 on v3

--- a/solution.py
+++ b/solution.py
@@ -1,4 +1,5 @@
 import functools
+import math
 
 import jax
 import jax.numpy as jnp
@@ -32,35 +33,39 @@
 
 
 class Comm:
-    def __init__(self, sizes, me, send, recv):
-        self.sizes, self.me, self.send, self.recv_sem = sizes, me, send, recv
-        self.copies = []
+    def __init__(self, sizes, me, sends, recv, zeros, dummy):
+        self.sizes, self.me, self.sends, self.recv_sem = sizes, me, sends, recv
+        self.zeros, self.dummy = zeros, dummy
+        self.copies, self.rows = [], 0
 
     def add(self, delta, src, dst):
-        slot = len(self.copies)
         device = tuple(i + d for i, d in zip(self.me, delta))
         copy = pltpu.make_async_remote_copy(
-            src_ref=src, dst_ref=dst, send_sem=self.send.at[slot], recv_sem=self.recv_sem.at[slot],
+            src_ref=src, dst_ref=dst, send_sem=self.sends[len(self.copies)], recv_sem=self.recv_sem,
             device_id=device, device_id_type=MESH,
         )
         to = inside(self.sizes, self.me, delta)
         source = inside(self.sizes, self.me, tuple(-d for d in delta))
         self.copies.append((copy, to, source, dst))
+        self.rows += math.prod(dst.shape) // 128
 
     def missing(self):
         for copy, to, source, dst in self.copies:
+            zero = next(z for z in self.zeros if z.shape[2] == dst.shape[-2])
+            n = dst.shape[-3] if len(dst.shape) > 2 else 1
+            zero = zero.at[:, 0:n] if len(dst.shape) == 4 else zero.at[0, 0:n] if len(dst.shape) == 3 else zero.at[0, 0]
 
             @pl.when(jnp.logical_not(source))
-            def _(dst=dst):
-                dst[...] = jnp.zeros(dst.shape, dst.dtype)
+            def _(dst=dst, zero=zero):
+                pltpu.make_async_copy(zero, dst, self.recv_sem).start()
 
     def start(self):
         for copy, to, source, dst in self.copies:
             pl.when(to)(copy.start)
 
-    def recv(self, first=0, last=None):
-        for copy, to, source, dst in self.copies[first:last]:
-            pl.when(source)(copy.wait_recv)
+    def recv(self):
+        all_rows = self.dummy.at[0 : self.rows]
+        pltpu.make_async_copy(all_rows, all_rows, self.recv_sem).wait()
 
     def sent(self):
         for copy, to, source, dst in self.copies:
@@ -79,10 +84,10 @@
         strips[1, :, i] = own[:, i, r - hy : r, :]
 
 
-def add_xy(comm, own, strips, bufs, dz=0):
+def add_xy(comm, own, strips, bufs, dz=0, deltas=XY):
     rx, ry, rc = bufs
     p, hx = own.shape[1], rx.shape[2]
-    for dx, dy in XY:
+    for dx, dy in deltas:
         xs = slice(0, hx) if dx < 0 else slice(p - hx, p)
         if dy == 0:
             src, dst = own.at[:, xs], rx.at[pick(-dx)]
@@ -158,7 +163,7 @@
 def kernel(sizes, vel_hbm, den_hbm, off_hbm, eig_hbm, new_vel, new_den, press, off, eig, fetch_sem, fields, stripA, rxA, ryA, rcA, mixed,
            edge, gotP, src, code, place, weight, resT, u, extU, packU, wide, s0, q0, r0,
            tmp0, own1, strip1, rx1, ry1, rc1, rz1, ext1, wide1, q1, r1, tmp1, own2, got2, ext2, sum1, fine,
-           sA, rA, szA, rzA, sB, rB, sC, rC, sD, rD, *bufB):
+           sends, recvs, z32, z16, z8, z4, z2, dummy, *bufB):
     me = tuple(lax.axis_index(a) for a in ("gx", "gy", "gz"))
     p, r = fields.shape[1], fields.shape[2]
     p1, r1n = p // 2, r // 2
@@ -167,6 +172,8 @@
     fetch = [pltpu.make_async_copy(a, b, fetch_sem.at[i]) for i, (a, b) in enumerate(pairs)]
     for copy in fetch:
         copy.start()
+    for zero in (z32, z16, z8, z4, z2):
+        zero[...] = jnp.zeros(zero.shape, jnp.float32)
 
     barrier = pltpu.get_barrier_semaphore()
     peers = [(dx, dy, dz) for dz in (-1, 0, 1) for dx in (-1, 0, 1) for dy in (-1, 0, 1) if (dx, dy, dz) != (0, 0, 0)]
@@ -180,20 +187,23 @@
 
         count = count + jnp.where(ok, 1, 0)
 
-    sendA = [Comm(sizes, me, sA.at[i], rA.at[i]) for i in range(3)]
+    made = []
+    zeros = [z32, z16, z8, z4, z2]
+
+    def comm(at):
+        sems = [sends.at[i] for i in range(at, sends.shape[0])]
+        made.append(Comm(sizes, me, sems, recvs.at[len(made)], zeros, dummy))
+        return made[-1]
+
+    commA = [comm(8 * c) for c in range(4)]
     for c in range(4):
-        for dx in (-1, 1):
-            xs = slice(0, HALO) if dx < 0 else slice(p - HALO, p)
-            sendA[0].add((dx, 0, 0), fields.at[c, xs], rxA.at[pick(-dx), c])
-            sendA[1].add((0, dx, 0), stripA.at[pick(dx), c], ryA.at[pick(-dx), c])
-            for dy in (-1, 1):
-                sendA[2].add((dx, dy, 0), stripA.at[pick(dy), c, xs], rcA.at[pick(-dx), pick(-dy), c])
-    zA = Comm(sizes, me, szA, rzA)
+        add_xy(commA[c], fields.at[c : c + 1], stripA.at[:, c : c + 1], (rxA.at[:, c : c + 1], ryA.at[:, c : c + 1], rcA.at[:, :, c : c + 1]))
+    zA = [comm(32) for c in range(4)]
     for c in range(4):
-        zA.add((0, 0, -1), edge.at[c], gotP.at[1, c])
-        zA.add((0, 0, 1), edge.at[c], gotP.at[0, c])
+        zA[c].add((0, 0, -1), edge.at[c], gotP.at[1, c])
+        zA[c].add((0, 0, 1), edge.at[c], gotP.at[0, c])
     fieldB = [bufB[8 * c : 8 * c + 8] for c in range(3)]
-    commB = [Comm(sizes, me, sB.at[c], rB.at[c]) for c in range(3)]
+    commB = [comm(0) for c in range(3)]
     for c, (strip, rx, ry, rc, edgeB, estrB, ezB, ezyB) in enumerate(fieldB):
         add_xy(commB[c], u.at[c : c + 1], strip, (rx, ry, rc))
         for dz in (-1, 1):
@@ -201,26 +211,32 @@
                 for dy in (-1, 1):
                     commB[c].add((dx, dy, dz), estrB.at[pick(dy)], ezyB.at[pick(-dz), 1 - dx, pick(-dy)])
                 commB[c].add((dx, 0, dz), edgeB, ezB.at[pick(-dz), 1 - dx])
-    commC = Comm(sizes, me, sC, rC)
-    commD = Comm(sizes, me, sD, rD)
+    commC = comm(0)
+    commD = comm(0)
     for dz in (-1, 1, 0):
-        add_xy(commC, own1, strip1, (rx1.at[1 - dz], ry1.at[1 - dz], rc1.at[1 - dz]), dz)
-        for dx, dy in XY:
+        add_xy(commC, own1, strip1, (rx1.at[1 - dz], ry1.at[1 - dz], rc1.at[1 - dz]), dz, XY[4:] if dz else XY)
+        for dx, dy in XY[4:] if dz else XY:
             commD.add((dx, dy, dz), own2, got2.at[1 - dz, 1 - dx, 1 - dy])
         if dz:
             commC.add((0, 0, dz), own1, rz1.at[pick(-dz)])
             commD.add((0, 0, dz), own2, got2.at[1 - dz, 1, 1])
-    comms = sendA + [zA] + commB + [commC, commD]
-    for comm in comms:
-        comm.missing()
+    for each in made[:8]:
+        each.missing()
+    for z in (0, 2):
+        rc1[z] = jnp.zeros(rc1.shape[1:], jnp.float32)
+        for x in (0, 2):
+            for y in (0, 2):
+                got2[z, x, y] = jnp.zeros(got2.shape[3:], jnp.float32)
     ext2[...] = jnp.zeros(ext2.shape, jnp.float32)
     sum1[...] = jnp.zeros(sum1.shape, jnp.float32)
     for copy in fetch[:2]:
         copy.wait()
     cut_strips(fields, stripA)
     pl.semaphore_wait(barrier, count)
-    for comm in sendA:
-        comm.start()
+    for each in commA:
+        each.start()
+    for each in made[8:]:
+        each.missing()
 
     even = ((lanes((8, 128)) >> 3) & 1) == 0
 
@@ -248,11 +264,10 @@
     half = r // 8
     lane16 = lanes((r, 128))
     lane = lanes((rows, 128))
-    near_steps = [[dy for dy in range(9) if 0 <= 8 * t + dy - 4 <= r - 8] for t in range(half)]
-    far_steps = [[dy for dy in range(9) if dy not in near_steps[t]] for t in range(half)]
-
-    def advect(c, t, b, steps):
-        return advect_block(place.at[t, b], weight.at[t, b], steps, lambda far, dy: src[c, b + far, 8 * t + 4 + dy : 8 * t + 12 + dy, :])
+
+    def advect(c, t, b):
+        totals = advect_block(place.at[t, b], weight.at[t, b], range(9), lambda far, dy: src[c, b + far, 8 * t + 4 + dy : 8 * t + 12 + dy, :])
+        resT[c, t, b] = totals
 
     def put(c, b, start, size, v):
         if b == 0:
@@ -260,29 +275,14 @@
         else:
             src[c, b, start : start + size] = v
 
-    def first(c, carry):
-        for dx in (-1, 1):
-            xs = slice(0, HALO) if dx < 0 else slice(p - HALO, p)
-            copy = pltpu.make_async_remote_copy(
-                src_ref=fields.at[c, xs], dst_ref=rxA.at[pick(-dx), c], send_sem=sA.at[0, 2 * c + pick(dx)],
-                recv_sem=rA.at[0, 2 * c + pick(dx)], device_id=tuple(i + d for i, d in zip(me, (dx, 0, 0))), device_id_type=MESH,
-            )
-            pl.when(inside(sizes, me, (-dx, 0, 0)))(copy.wait_recv)
+    low = (lanes((r + 16, 128)) & 7) < 4
+    for c in range(4):
+        commA[c].recv()
         for t in range(half):
             ys = slice(8 * t, 8 * t + 8)
             planes = [rxA[0, c, x, ys] for x in range(HALO)] + [fields[c, x, ys] for x in range(p)] + [rxA[1, c, x, ys] for x in range(HALO)]
             for b, v in enumerate(swap_blocks(planes, 8, 4)):
                 put(c, b, 8 + 8 * t, 8, v)
-        for b in range(1, blocks - 1):
-            for t in range(half):
-                resT[c, t, b] = advect(c, t, b, near_steps[t])
-        return carry
-
-    lax.fori_loop(0, 4, first, 0)
-    sendA[1].recv()
-    sendA[2].recv()
-
-    def turn(c, carry):
         for side, at in ((1, 0), (0, 4)):
             for x in range(HALO):
                 mixed[c, x, at : at + 4] = rcA[0, side, c, x]
@@ -292,21 +292,18 @@
         for b, v in enumerate(swap_blocks([mixed[c, x] for x in range(p + 8)], 8, 4)):
             put(c, b, 4, 4, v[4:8])
             put(c, b, r + 8, 4, v[0:4])
-        return carry
-
-    lax.fori_loop(0, 4, turn, 0)
-    zA.start()
-    low = (lanes((r + 16, 128)) & 7) < 4
-    for c in range(4):
+        if c:
+            zA[c - 1].sent()
+        zA[c].start()
         for b in range(1, blocks - 1):
             for t in range(half):
-                resT[c, t, b] = resT[c, t, b] + advect(c, t, b, far_steps[t])
-        zA.recv(2 * c, 2 * c + 2)
+                advect(c, t, b)
+        zA[c].recv()
         src[c, 0] = jnp.where(low, gotP[0, c], edge[c])
         src[c, blocks] = jnp.where(low, edge[c], gotP[1, c])
         for b in (0, blocks - 1):
             for t in range(half):
-                resT[c, t, b] = advect(c, t, b, range(9))
+                advect(c, t, b)
         for t in range(half):
             pairs = []
             for q in range(blocks // 2):
@@ -326,9 +323,13 @@
         edgeB[...] = total
         estrB[0] = total[0 : estrB.shape[1]]
         estrB[1] = total[r - estrB.shape[1] : r]
+        for each in commB[c - 1 : c] if c else commA:
+            each.sent()
         commB[c].start()
 
     extU[:, HALO : HALO + p, HALO : HALO + r, :] = u[0:3]
+    zA[3].sent()
+    commB[2].sent()
     for c in range(3):
         commB[c].recv()
 
@@ -403,6 +404,7 @@
 
     cut_strips(own1, strip1)
     commC.start()
+    commC.sent()
     commC.recv()
     rows1 = r1n + 8
     for dz in range(3):
@@ -426,6 +428,7 @@
 
     commD.start()
     got2[1, 1, 1] = own2[...]
+    commD.sent()
     commD.recv()
     for z in range(3):
         for a in range(3):
@@ -463,8 +466,6 @@
         new_vel[0, x] = u[0, x] - 0.5 * cut(s0[x + HALO + 1] - s0[x + HALO - 1])
         new_vel[1, x] = u[1, x] - 0.5 * cut(roll(v, -1, 0) - roll(v, 1, 0))
         new_vel[2, x] = u[2, x] - 0.5 * cut(roll(v, -1, 1) - roll(v, 1, 1))
-    for comm in comms:
-        comm.sent()
 
 
 def write_kernel(*refs):
@@ -513,7 +514,7 @@
         + [vm(3, 1, p1 + 8, rows1, 128), vm(p1 + 8, rows1, 256), vm(p1 + 8, rows1, 256),
            vm(p1 + 8, rows1, 128), vm(rows1, 128), vm(p2, r2, 128), vm(3, 3, 3, p2, r2, 128), vm(3, 3 * p2, 16, 128),
            vm(3 * p2, 2, rows1, 128), vm(p1 + 8, 2, rows, 128)]
-        + [dma(3, 16), dma(3, 16), dma(8), dma(8), dma(3, 26), dma(3, 26)] + [dma(26), dma(26)] * 2
+        + [dma(34), dma(13), vm(1, 1, r + 16, 128), vm(1, 4, r, 128), vm(1, 4, 8, 128), vm(1, 8, 4, 128), vm(1, 8, 2, 128), vm(512, 128)]
     )
     for hx, hy in ((3, 2), (2, 4), (2, 2)):
         scratch += xy(1, p, r, hx, hy) + [vm(r, 128), vm(2, hy, 128), vm(2, 3, r, 128), vm(2, 3, 2, hy, 128)]

time: 36.8 us -> 31.8 us (0.86)
  Pallas kernels: 36.1 us -> 31 us
    pallas_call x1, Pallas kernels: 35.3 us -> 30.2 us  [step(): pl.pallas_call(functools.partial(kernel, sizes), out_shape=(jax.ShapeDtyp...]
where the time goes in v4:
time: 31.8 us; the launch traced here: 31.6 us
  Pallas kernels  31 us (97%)
  between operations  0.64 us (2%)
    pallas_call x1, Pallas kernels, step(): pl.pallas_call(functools.partial(kernel, sizes), out_shape=(jax.ShapeDtyp...  30.2 us
    pallas_call x1, Pallas kernels, write_out(): pl.pallas_call(write_kernel, out_shape=tuple((jax.ShapeDtypeStruct(a.shap...  0.74 us

profile of v4, /device:TPU:0, one launch (start us, length us, event | category | flops | bytes accessed | tf_op | source)
XLA Modules:
  0.0 31.6 jit_solution(6080090205532557978)
XLA Ops:
  0.6 30.2 %shard_map.67 = (f32[3,8,16,128]{3,2,1,0:T(8,128)S(1)}, f32[8,16,128]{2,1,0:T(8,128)S(1)}, f32[8,16,128]{2,1,0:T(8,128)S(1)}) custom-call(f32[3,8,16,128]{3,2,1,0:T(8,128)} %vel_hbm.1, f32[8,16,128]{2,1,0:T(8,128)} %den_hbm.1, s32[3,8,16,128]{3,2,1,0:T(8,128)} %off_hbm.1, s32[3,8,16,128]{3,2,1,0:T(8,128)} %eig_hbm.1), custom_call_target="tpu_custom_call" | custom-call | tf_op jit(solution)/shard_map/pallas_call | solution.py:522
  30.9 0.7 %shard_map.68 = (f32[3,8,16,128]{3,2,1,0:T(8,128)}, f32[8,16,128]{2,1,0:T(8,128)}, f32[8,16,128]{2,1,0:T(8,128)}) custom-call(f32[3,8,16,128]{3,2,1,0:T(8,128)S(1)} %get-tuple-element.6.refs_0_, f32[8,16,128]{2,1,0:T(8,128)S(1)} %get-tuple-element.7.refs_1_, f32[8,16,128]{2,1,0:T(8,128)S(1)} %get-tuple-element.8.refs_2_), custom_call_target="tpu_custom_call" | custom-call | tf_op jit(solution)/shard_map/pallas_call | solution.py:481

commit v5 on v4

--- a/solution.py
+++ b/solution.py
@@ -172,9 +172,6 @@
     fetch = [pltpu.make_async_copy(a, b, fetch_sem.at[i]) for i, (a, b) in enumerate(pairs)]
     for copy in fetch:
         copy.start()
-    for zero in (z32, z16, z8, z4, z2):
-        zero[...] = jnp.zeros(zero.shape, jnp.float32)
-
     barrier = pltpu.get_barrier_semaphore()
     peers = [(dx, dy, dz) for dz in (-1, 0, 1) for dx in (-1, 0, 1) for dy in (-1, 0, 1) if (dx, dy, dz) != (0, 0, 0)]
     count = jnp.int32(0)
@@ -187,6 +184,8 @@
 
         count = count + jnp.where(ok, 1, 0)
 
+    for zero in (z32, z16, z8, z4, z2):
+        zero[...] = jnp.zeros(zero.shape, jnp.float32)
     made = []
     zeros = [z32, z16, z8, z4, z2]
 
@@ -330,24 +329,11 @@
     extU[:, HALO : HALO + p, HALO : HALO + r, :] = u[0:3]
     zA[3].sent()
     commB[2].sent()
-    for c in range(3):
-        commB[c].recv()
 
     def edges(lo, hi):
         spot = lanes(lo[0].shape)
         v = [jnp.where((spot & 7) < 4, lo[i], hi[i]) for i in range(3)]
         return jnp.where(spot < 32, roll(v[0], -32, 1), jnp.where(spot < 96, roll(v[1], 32, 1), roll(v[2], 96, 1)))
-
-    for c, (strip, rx, ry, rc, edgeB, estrB, ezB, ezyB) in enumerate(fieldB):
-        frame_halo((rx, ry, rc), p, r, extU.at[c : c + 1])
-        hy = estrB.shape[1]
-        packU[c, HALO : HALO + r] = edges([ezB[0, i] for i in range(3)], [ezB[1, i] for i in range(3)])
-        for sy, ys in ((0, slice(HALO - hy, HALO)), (1, slice(HALO + r, HALO + r + hy))):
-            packU[c, ys] = edges([ezyB[0, i, sy] for i in range(3)], [ezyB[1, i, sy] for i in range(3)])
-    for c in range(3):
-        for x in range(HALO - 3, HALO + p + 3):
-            wide[c, x, :, 0:128] = extU[c, x]
-            wide[c, x, :, 128:256] = roll(packU[c], -(8 * x + 4), 1)
 
     def yz_mask(nrows, first_row, block_rows, cells):
         row = lax.broadcasted_iota(jnp.int32, (nrows, 256), 0) - first_row + me[1] * block_rows
@@ -373,28 +359,32 @@
         first = (RELAX * scale) * v
         return first + RELAX * (scale * v - (RELAX * scale) * around(ref, x, step))
 
-    def source0(x, carry):
-        part = wide[0, x + 1] - wide[0, x - 1]
-        v = wide[1, x]
-        part = part + (roll(v, -1, 0) - roll(v, 1, 0))
-        v = wide[2, x]
-        part = part + (roll(v, -1, 1) - roll(v, 1, 1))
-        s0[x] = jnp.where(mask0 & x_ok(x, HALO, p), -0.5 * part, 0.0)
-        return carry
-
-    lax.fori_loop(HALO - 2, HALO + p + 2, source0, 0)
-
-    def second0(x, carry):
+    for c, (strip, rx, ry, rc, edgeB, estrB, ezB, ezyB) in enumerate(fieldB):
+        commB[c].recv()
+        frame_halo((rx, ry, rc), p, r, extU.at[c : c + 1])
+        hy = estrB.shape[1]
+        packU[c, HALO : HALO + r] = edges([ezB[0, i] for i in range(3)], [ezB[1, i] for i in range(3)])
+        for sy, ys in ((0, slice(HALO - hy, HALO)), (1, slice(HALO + r, HALO + r + hy))):
+            packU[c, ys] = edges([ezyB[0, i, sy] for i in range(3)], [ezyB[1, i, sy] for i in range(3)])
+        side = packU[c]
+        for x in range(HALO - 3, HALO + p + 3):
+            wide[c, x, :, 0:128] = extU[c, x]
+            wide[c, x, :, 128:256] = roll(side, -(8 * x + 4), 1)
+        for x in range(HALO - 2, HALO + p + 2):
+            if c == 0:
+                s0[x] = wide[0, x + 1] - wide[0, x - 1]
+            elif c == 1:
+                v = wide[1, x]
+                s0[x] = s0[x] + (roll(v, -1, 0) - roll(v, 1, 0))
+            else:
+                v = wide[2, x]
+                part = s0[x] + (roll(v, -1, 1) - roll(v, 1, 1))
+                s0[x] = jnp.where(mask0 & x_ok(x, HALO, p), -0.5 * part, 0.0)
+
+    for x in range(HALO - 1, HALO + p + 1):
         q0[x] = jnp.where(mask0 & x_ok(x, HALO, p), second(s0, x, 1.0, 1), 0.0)
-        return carry
-
-    lax.fori_loop(HALO - 1, HALO + p + 1, second0, 0)
-
-    def residual0(x, carry):
+    for x in range(HALO, HALO + p):
         r0[x] = (s0[x] - around(q0, x, 1))[:, 0:128]
-        return carry
-
-    lax.fori_loop(HALO, HALO + p, residual0, 0)
     lane8 = lanes((r // 2, 128))
     for x in range(p // 2):
         tmp0[...] = r0[HALO + 2 * x] + r0[HALO + 2 * x + 1]

time: 31.8 us -> 29.5 us (0.928)
  Pallas kernels: 31 us -> 28.7 us
    pallas_call x1, Pallas kernels: 30.2 us -> 28 us  [step(): pl.pallas_call(functools.partial(kernel, sizes), out_shape=(jax.ShapeDtyp...]
where the time goes in v5:
time: 29.5 us; the launch traced here: 29.4 us
  Pallas kernels  28.7 us (97%)
  between operations  0.64 us (2%)
    pallas_call x1, Pallas kernels, step(): pl.pallas_call(functools.partial(kernel, sizes), out_shape=(jax.ShapeDtyp...  28 us
    pallas_call x1, Pallas kernels, write_out(): pl.pallas_call(write_kernel, out_shape=tuple((jax.ShapeDtypeStruct(a.shap...  0.74 us

profile of v5, /device:TPU:0, one launch (start us, length us, event | category | flops | bytes accessed | tf_op | source)
XLA Modules:
  0.0 29.4 jit_solution(7012831026867980985)
XLA Ops:
  0.6 28.0 %shard_map.67 = (f32[3,8,16,128]{3,2,1,0:T(8,128)S(1)}, f32[8,16,128]{2,1,0:T(8,128)S(1)}, f32[8,16,128]{2,1,0:T(8,128)S(1)}) custom-call(f32[3,8,16,128]{3,2,1,0:T(8,128)} %vel_hbm.1, f32[8,16,128]{2,1,0:T(8,128)} %den_hbm.1, s32[3,8,16,128]{3,2,1,0:T(8,128)} %off_hbm.1, s32[3,8,16,128]{3,2,1,0:T(8,128)} %eig_hbm.1), custom_call_target="tpu_custom_call" | custom-call | tf_op jit(solution)/shard_map/pallas_call | solution.py:512
  28.6 0.7 %shard_map.68 = (f32[3,8,16,128]{3,2,1,0:T(8,128)}, f32[8,16,128]{2,1,0:T(8,128)}, f32[8,16,128]{2,1,0:T(8,128)}) custom-call(f32[3,8,16,128]{3,2,1,0:T(8,128)S(1)} %get-tuple-element.6.refs_0_, f32[8,16,128]{2,1,0:T(8,128)S(1)} %get-tuple-element.7.refs_1_, f32[8,16,128]{2,1,0:T(8,128)S(1)} %get-tuple-element.8.refs_2_), custom_call_target="tpu_custom_call" | custom-call | tf_op jit(solution)/shard_map/pallas_call | solution.py:471

commit v6 on v5

--- a/solution.py
+++ b/solution.py
@@ -309,6 +309,8 @@
                 one, two = resT[c, t, 2 * q], resT[c, t, 2 * q + 1]
                 move = jnp.where(even, two, one)
                 pairs.append(jnp.where(even, one, two) + jnp.where(even, roll(move, -8, 1), roll(move, 8, 1)))
+            if c < 3:
+                fieldB[c][4][8 * t : 8 * t + 8] = jnp.where(even, pairs[0], pairs[-1])
             for x, v in enumerate(swap_blocks(pairs, 16)):
                 u[c, x, 8 * t : 8 * t + 8] = v
         if c == 3:
@@ -316,12 +318,9 @@
             break
         strip, rx, ry, rc, edgeB, estrB, ezB, ezyB = fieldB[c]
         cut_strips(u.at[c : c + 1], strip)
-        total = roll(u[c, 0], 4, 1)
-        for x in range(1, p):
-            total = jnp.where(lane16 >= 8 * x, roll(u[c, x], 4 + 8 * x, 1), total)
-        edgeB[...] = total
-        estrB[0] = total[0 : estrB.shape[1]]
-        estrB[1] = total[r - estrB.shape[1] : r]
+        hy = estrB.shape[1]
+        estrB[0] = edgeB[0:hy]
+        estrB[1] = edgeB[r - hy : r]
         for each in commB[c - 1 : c] if c else commA:
             each.sent()
         commB[c].start()
@@ -331,9 +330,7 @@
     commB[2].sent()
 
     def edges(lo, hi):
-        spot = lanes(lo[0].shape)
-        v = [jnp.where((spot & 7) < 4, lo[i], hi[i]) for i in range(3)]
-        return jnp.where(spot < 32, roll(v[0], -32, 1), jnp.where(spot < 96, roll(v[1], 32, 1), roll(v[2], 96, 1)))
+        return jnp.where((lanes(lo.shape) & 15) < 8, hi, roll(lo, -16, 1))
 
     def yz_mask(nrows, first_row, block_rows, cells):
         row = lax.broadcasted_iota(jnp.int32, (nrows, 256), 0) - first_row + me[1] * block_rows
@@ -363,13 +360,14 @@
         commB[c].recv()
         frame_halo((rx, ry, rc), p, r, extU.at[c : c + 1])
         hy = estrB.shape[1]
-        packU[c, HALO : HALO + r] = edges([ezB[0, i] for i in range(3)], [ezB[1, i] for i in range(3)])
-        for sy, ys in ((0, slice(HALO - hy, HALO)), (1, slice(HALO + r, HALO + r + hy))):
-            packU[c, ys] = edges([ezyB[0, i, sy] for i in range(3)], [ezyB[1, i, sy] for i in range(3)])
-        side = packU[c]
+        for i in range(3):
+            packU[c, i, HALO : HALO + r] = edges(ezB[0, i], ezB[1, i])
+            for sy, ys in ((0, slice(HALO - hy, HALO)), (1, slice(HALO + r, HALO + r + hy))):
+                packU[c, i, ys] = edges(ezyB[0, i, sy], ezyB[1, i, sy])
         for x in range(HALO - 3, HALO + p + 3):
             wide[c, x, :, 0:128] = extU[c, x]
-            wide[c, x, :, 128:256] = roll(side, -(8 * x + 4), 1)
+            i = 0 if x < HALO else 1 if x < HALO + p else 2
+            wide[c, x, :, 128:256] = roll(packU[c, i], -16 * ((x - HALO) % p), 1)
         for x in range(HALO - 2, HALO + p + 2):
             if c == 0:
                 s0[x] = wide[0, x + 1] - wide[0, x - 1]
@@ -498,7 +496,7 @@
         + [vm(4, p + 8, 8, 128), vm(4, r + 16, 128), vm(2, 4, r + 16, 128), vm(4, 17, r + 16, 128),
            pltpu.VMEM((p, r, 128), jnp.int32), pltpu.VMEM((half, 16, 2, 8, 128), jnp.int32), vm(half, 16, 11, 8, 128),
            vm(4, half, 16, 8, 128), vm(4, p, r, 128)]
-        + [vm(3, p + 8, rows, 128), vm(3, rows, 128), vm(3, p + 8, rows, 256),
+        + [vm(3, p + 8, rows, 128), vm(3, 3, rows, 128), vm(3, p + 8, rows, 256),
            vm(p + 8, rows, 256), vm(p + 8, rows, 256), vm(p + 8, rows, 128), vm(rows, 128), vm(1, p1, r1, 128)]
         + [vm(2, 1, p1, 2, 128), vm(3, 2, 1, 2, r1, 128), vm(3, 2, 1, p1, 2, 128), vm(3, 2, 2, 1, 2, 2, 128), vm(2, 1, p1, r1, 128)]
         + [vm(3, 1, p1 + 8, rows1, 128), vm(p1 + 8, rows1, 256), vm(p1 + 8, rows1, 256),

time: 29.5 us -> 29.2 us (0.990)
  Pallas kernels: 28.7 us -> 28.4 us
    pallas_call x1, Pallas kernels: 28 us -> 27.6 us  [step(): pl.pallas_call(functools.partial(kernel, sizes), out_shape=(jax.ShapeDtyp...]
where the time goes in v6:
time: 29.2 us; the launch traced here: 29 us
  Pallas kernels  28.4 us (97%)
  between operations  0.64 us (2%)
    pallas_call x1, Pallas kernels, step(): pl.pallas_call(functools.partial(kernel, sizes), out_shape=(jax.ShapeDtyp...  27.6 us
    pallas_call x1, Pallas kernels, write_out(): pl.pallas_call(write_kernel, out_shape=tuple((jax.ShapeDtypeStruct(a.shap...  0.74 us

profile of v6, /device:TPU:0, one launch (start us, length us, event | category | flops | bytes accessed | tf_op | source)
XLA Modules:
  0.0 29.0 jit_solution(514089810896691200)
XLA Ops:
  0.6 27.6 %shard_map.67 = (f32[3,8,16,128]{3,2,1,0:T(8,128)S(1)}, f32[8,16,128]{2,1,0:T(8,128)S(1)}, f32[8,16,128]{2,1,0:T(8,128)S(1)}) custom-call(f32[3,8,16,128]{3,2,1,0:T(8,128)} %vel_hbm.1, f32[8,16,128]{2,1,0:T(8,128)} %den_hbm.1, s32[3,8,16,128]{3,2,1,0:T(8,128)} %off_hbm.1, s32[3,8,16,128]{3,2,1,0:T(8,128)} %eig_hbm.1), custom_call_target="tpu_custom_call" | custom-call | tf_op jit(solution)/shard_map/pallas_call | solution.py:510
  28.3 0.7 %shard_map.68 = (f32[3,8,16,128]{3,2,1,0:T(8,128)}, f32[8,16,128]{2,1,0:T(8,128)}, f32[8,16,128]{2,1,0:T(8,128)}) custom-call(f32[3,8,16,128]{3,2,1,0:T(8,128)S(1)} %get-tuple-element.6.refs_0_, f32[8,16,128]{2,1,0:T(8,128)S(1)} %get-tuple-element.7.refs_1_, f32[8,16,128]{2,1,0:T(8,128)S(1)} %get-tuple-element.8.refs_2_), custom_call_target="tpu_custom_call" | custom-call | tf_op jit(solution)/shard_map/pallas_call | solution.py:469

commit v7 on v6

--- a/solution.py
+++ b/solution.py
@@ -204,15 +204,19 @@
     fieldB = [bufB[8 * c : 8 * c + 8] for c in range(3)]
     commB = [comm(0) for c in range(3)]
     for c, (strip, rx, ry, rc, edgeB, estrB, ezB, ezyB) in enumerate(fieldB):
+        for dx, dy in XY[:4]:
+            for dz in (-1, 1):
+                commB[c].add((dx, dy, dz), estrB.at[pick(dy)], ezyB.at[pick(-dz), 1 - dx, pick(-dy)])
         add_xy(commB[c], u.at[c : c + 1], strip, (rx, ry, rc))
         for dz in (-1, 1):
-            for dx in (-1, 1, 0):
-                for dy in (-1, 1):
-                    commB[c].add((dx, dy, dz), estrB.at[pick(dy)], ezyB.at[pick(-dz), 1 - dx, pick(-dy)])
+            for dx in (-1, 1):
                 commB[c].add((dx, 0, dz), edgeB, ezB.at[pick(-dz), 1 - dx])
+            for dy in (-1, 1):
+                commB[c].add((0, dy, dz), estrB.at[pick(dy)], ezyB.at[pick(-dz), 1, pick(-dy)])
+            commB[c].add((0, 0, dz), edgeB, ezB.at[pick(-dz), 1])
     commC = comm(0)
     commD = comm(0)
-    for dz in (-1, 1, 0):
+    for dz in (0, -1, 1):
         add_xy(commC, own1, strip1, (rx1.at[1 - dz], ry1.at[1 - dz], rc1.at[1 - dz]), dz, XY[4:] if dz else XY)
         for dx, dy in XY[4:] if dz else XY:
             commD.add((dx, dy, dz), own2, got2.at[1 - dz, 1 - dx, 1 - dy])

time: 29.2 us -> 29.1 us (level)
  no operation moved by 1% of the time
where the time goes in v7:
time: 29.1 us; the launch traced here: 28.9 us
  Pallas kernels  28.3 us (97%)
  between operations  0.64 us (2%)
    pallas_call x1, Pallas kernels, step(): pl.pallas_call(functools.partial(kernel, sizes), out_shape=(jax.ShapeDtyp...  27.5 us
    pallas_call x1, Pallas kernels, write_out(): pl.pallas_call(write_kernel, out_shape=tuple((jax.ShapeDtypeStruct(a.shap...  0.74 us

profile of v7, /device:TPU:0, one launch (start us, length us, event | category | flops | bytes accessed | tf_op | source)
XLA Modules:
  0.0 28.9 jit_solution(16802355512587521009)
XLA Ops:
  0.6 27.5 %shard_map.67 = (f32[3,8,16,128]{3,2,1,0:T(8,128)S(1)}, f32[8,16,128]{2,1,0:T(8,128)S(1)}, f32[8,16,128]{2,1,0:T(8,128)S(1)}) custom-call(f32[3,8,16,128]{3,2,1,0:T(8,128)} %vel_hbm.1, f32[8,16,128]{2,1,0:T(8,128)} %den_hbm.1, s32[3,8,16,128]{3,2,1,0:T(8,128)} %off_hbm.1, s32[3,8,16,128]{3,2,1,0:T(8,128)} %eig_hbm.1), custom_call_target="tpu_custom_call" | custom-call | tf_op jit(solution)/shard_map/pallas_call | solution.py:514
  28.2 0.7 %shard_map.68 = (f32[3,8,16,128]{3,2,1,0:T(8,128)}, f32[8,16,128]{2,1,0:T(8,128)}, f32[8,16,128]{2,1,0:T(8,128)}) custom-call(f32[3,8,16,128]{3,2,1,0:T(8,128)S(1)} %get-tuple-element.6.refs_0_, f32[8,16,128]{2,1,0:T(8,128)S(1)} %get-tuple-element.7.refs_1_, f32[8,16,128]{2,1,0:T(8,128)S(1)} %get-tuple-element.8.refs_2_), custom_call_target="tpu_custom_call" | custom-call | tf_op jit(solution)/shard_map/pallas_call | solution.py:473
